TPU v7x, 32 devices: a whole 2x2x4 slice. The times are simulated.
32 devices in a mesh: dp: 8 (over z, y), mp: 4 (over x, core).
Axes of the slice: x: 2, y: 2, z: 4, core: 2. Of those that a mesh axis runs over, the one named last changes fastest.
Arguments:
- hidden: bfloat16 [1024, 7168], P('dp', 'mp'), may hold values from -40 to 40
- live: int32 [1024], P('dp'), may hold values 0 or 1
- norm_gain: float32 [7168], replicated, may hold values from 0.25 to 1.75
- q_weight: bfloat16 [7168, 1536], P(None, 'mp'), may hold values from -0.28347335 to 0.28347335
- kv_weight: bfloat16 [7168, 512], P(None, 'mp'), may hold values from -0.28347335 to 0.28347335
- ratio_ids: int32 [4], replicated, may hold values from 0 to 19
Outputs:
- losses: float32 [4], replicated
- q_latent: bfloat16 [1024, 1536], P('dp', 'mp')
- kv_latent: bfloat16 [1024, 512], P('dp', 'mp')
- feature_means: float32 [7168], replicated
All inputs are finite; a program needn't handle non-finite values. No bound on the sum of `live` on one device may be relied on, other than what follows from the above.
Results may differ from a plain program's by a relative error of at most 0.0052.
Values may be sent and summed in bfloat16 or wider, within the bound.
No kernel may reach another device: no remote copies, remote signals or barrier semaphores. Data moves between devices by JAX's collectives and lax.ppermute only.
A program may use at most 256 MiB of HBM per device.

v0:
```python
import jax
import jax.numpy as jnp
from jax import lax
from jax.sharding import PartitionSpec as P

GROUP = 128
GRID = 20
RATIOS = 4


def fake_quant(weights, scales):
    height, columns = weights.shape
    scaled = weights.astype(jnp.float32) * scales[:, None]
    grouped = scaled.reshape(height // GROUP, GROUP, columns)
    unit_size = (jnp.max(jnp.abs(grouped), axis=1, keepdims=True) + 1e-06) / 7.0
    levels = grouped / unit_size
    stairs = (levels - jnp.sin(2.0 * jnp.pi * levels) / (2.0 * jnp.pi)) * unit_size
    return (stairs.reshape(height, columns) / scales[:, None]).astype(jnp.bfloat16)


def stack_weights(weights, totals, ratio_ids):
    logged = jnp.log(totals + 1e-06)
    centred = logged - 0.5 * (jnp.max(logged) + jnp.min(logged))
    alphas = ratio_ids.astype(jnp.float32) / GRID
    scales = jnp.exp(alphas[:, None] * centred[None, :])
    members = [weights]
    for position in range(RATIOS):
        members.append(fake_quant(weights, scales[position]))
    return jnp.stack(members)


def per_device(hidden, live, norm_gain, q_weight, kv_weight, ratio_ids):
    weights = jnp.concatenate([q_weight, kv_weight], axis=1)
    live_rows = live.astype(jnp.float32)[:, None]
    values = hidden.astype(jnp.float32)
    slice_width = hidden.shape[1]
    row_square = lax.psum(jnp.sum(values * values, axis=1), "mp")
    full_width = slice_width * lax.axis_size("mp")
    offset = lax.axis_index("mp") * slice_width
    gain_slice = lax.dynamic_slice_in_dim(norm_gain, offset, slice_width)
    scaling = lax.rsqrt(row_square[:, None] / full_width + 1e-06)
    normed = (values * scaling * gain_slice[None, :]).astype(jnp.bfloat16)
    local_totals = jnp.sum(jnp.abs(normed.astype(jnp.float32)) * live_rows, axis=0)
    slice_sums = lax.psum(local_totals, "dp")
    totals = lax.all_gather(slice_sums, "mp", axis=0, tiled=True)
    stacked = stack_weights(weights, totals, ratio_ids)
    products = jnp.einsum(
        "tk,rkc->rtc",
        lax.all_gather(normed, "mp", axis=1, tiled=True),
        stacked,
        preferred_element_type=jnp.float32,
    )
    exact = products[0]
    approxes = products[1:]
    errors = jnp.sum(((approxes - exact[None]) * live_rows[None]) ** 2, axis=(1, 2))
    energy = jnp.sum((exact * live_rows) ** 2)
    errors, energy = lax.psum((errors, energy), ("dp", "mp"))
    losses = errors / energy
    inverse = 1.0 / (losses * losses)
    shares = inverse / jnp.sum(inverse)
    blended = jnp.zeros_like(exact)
    for position in range(RATIOS):
        blended = blended + shares[position] * approxes[position]
    blended = blended.astype(jnp.bfloat16)
    query_cols = q_weight.shape[1]
    token_count = hidden.shape[0] * lax.axis_size("dp")
    feature_means = totals / token_count
    return (losses, blended[:, :query_cols], blended[:, query_cols:], feature_means)


def solution(mesh):
    placed = (P("dp", "mp"), P("dp"), P(), P(None, "mp"), P(None, "mp"), P())
    return jax.shard_map(
        per_device,
        mesh=mesh,
        in_specs=placed,
        out_specs=(P(), P("dp", "mp"), P("dp", "mp"), P()),
        check_vma=False,
    )
```

profile of v0, /device:TPU:0, one launch (start us, length us, event | category | flops | bytes accessed | tf_op | source)
XLA Modules:
  0.0 463.1 jit_solution(13123839531616765572)
XLA Ops:
  7.2 0.0 all-gather.3.cloned.1.call-start
  7.2 0.7 convert_element_type.96
  7.9 1.2 fusion.25
  9.1 8.4 %psum.28 = f32[128]{0:T(128)S(1)} all-reduce(f32[128]{0:T(128)S(1)} %fusion.25), channel_id=1, replica_groups=mesh['dp'=8,'mp'=4] {'mp'}, use_global_device_ids=true, to_apply=%region_1.0 | all-reduce | flops 128 | bytes 1024 | tf_op jit(solution)/shard_map/psum | solution.py:37
  17.4 0.8 dynamic_slice.3
  18.2 2.1 multiply_reduce_fusion
  20.3 0.0 all-gather.3.cloned.1.call-update
  20.3 21.9 %psum.29 = f32[1792]{0:T(1024)S(1)} all-reduce(f32[1792]{0:T(1024)S(1)} %get-tuple-element.22), channel_id=1, replica_groups=mesh['dp'=8,'mp'=4] {'dp'}, use_global_device_ids=true, to_apply=%region_3.0 | all-reduce | flops 1792 | bytes 14336 | tf_op jit(solution)/shard_map/psum | solution.py:44
  42.3 5.2 %all-gather = f32[4,1,1792]{2,1,0:T(1,128)S(1)} all-gather(f32[1,1,1792]{2,1,0:T(1,128)S(1)} %reshape.526), channel_id=1, replica_groups=mesh['dp'=8,'mp'=4] {'mp'}, dimensions={0}, use_global_device_ids=true | all-gather | bytes 35840 | tf_op jit(solution)/shard_map/all_gather | solution.py:45
  47.5 1.3 fusion.33
  50.1 0.7 convert_multiply_fusion.10
  50.8 0.1 multiply_exponential_fusion
  50.9 0.1 fusion.36
  51.0 8.3 %copy.16 = bf16[7168,384]{0,1:T(8,128)(2,1)} copy(bf16[7168,384]{1,0:T(8,128)(2,1)} %param.9) | data formatting | bytes 11010048 | tf_op args[3]
  59.3 2.8 copy.17
  62.0 9.5 %fusion.11 = (f32[56,512]{1,0:T(8,128)S(1)}, f32[56,512]{1,0:T(8,128)S(1)}, f32[56,512]{1,0:T(8,128)S(1)}, f32[56,512]{1,0:T(8,128)S(1)}) fusion(f32[56,128]{1,0:T(8,128)S(1)} %bitcast.60, bf16[56,128,128]{2,1,0:T(8,128)(2,1)} %bitcast.59, bf16[56,128,384]{2,1,0:T(8,128)(2,1)} %bitcast.58, f32[56,128]{1,0:T(8,128)S(1)} %bitcast.62, ...), kind=kLoop, calls=%fused_computation.19 | loop fusion | flops 58605568 | bytes 7913472 | tf_op jit(solution)/shard_map/reduce_max | solution.py:15
  71.6 0.1 copy.20
  71.7 8.7 %div.182 = f32[56,128,512]{1,0,2:T(8,128)} broadcast(f32[56,512]{0,1:T(8,128)S(1)} %copy.20), dimensions={0,2} | broadcast | bytes 14794752 | tf_op jit(solution)/shard_map/div | solution.py:16
  80.4 16.0 %div.183 = f32[1,7168,512]{1,2,0:T(8,128)} reshape(f32[56,128,512]{1,0,2:T(8,128)} %div.182) | data formatting | bytes 29360128 | tf_op jit(solution)/shard_map/div | solution.py:16
  96.5 0.1 copy.21
  96.6 8.7 %div.188 = f32[56,128,512]{1,0,2:T(8,128)} broadcast(f32[56,512]{0,1:T(8,128)S(1)} %copy.21), dimensions={0,2} | broadcast | bytes 14794752 | tf_op jit(solution)/shard_map/div | solution.py:16
  105.3 16.0 %div.189 = f32[1,7168,512]{1,2,0:T(8,128)} reshape(f32[56,128,512]{1,0,2:T(8,128)} %div.188) | data formatting | bytes 29360128 | tf_op jit(solution)/shard_map/div | solution.py:16
  121.3 0.1 copy.22
  121.4 8.7 %div.194 = f32[56,128,512]{1,0,2:T(8,128)} broadcast(f32[56,512]{0,1:T(8,128)S(1)} %copy.22), dimensions={0,2} | broadcast | bytes 14794752 | tf_op jit(solution)/shard_map/div | solution.py:16
  130.1 16.1 %div.195 = f32[1,7168,512]{1,2,0:T(8,128)} reshape(f32[56,128,512]{1,0,2:T(8,128)} %div.194) | data formatting | bytes 29360128 | tf_op jit(solution)/shard_map/div | solution.py:16
  146.2 0.1 copy.23
  146.3 8.7 %div.200 = f32[56,128,512]{1,0,2:T(8,128)} broadcast(f32[56,512]{0,1:T(8,128)S(1)} %copy.23), dimensions={0,2} | broadcast | bytes 14794752 | tf_op jit(solution)/shard_map/div | solution.py:16
  155.0 16.0 %div.201 = f32[1,7168,512]{1,2,0:T(8,128)} reshape(f32[56,128,512]{1,0,2:T(8,128)} %div.200) | data formatting | bytes 29360128 | tf_op jit(solution)/shard_map/div | solution.py:16
  171.0 0.0 slice-start
  171.0 6.1 %fusion.16 = bf16[5,7168,512]{1,2,0:T(8,128)(2,1)} fusion(bf16[7168,128]{0,1:T(8,128)(2,1)S(1)} %copy.17, bf16[7168,384]{0,1:T(8,128)(2,1)} %copy.16), kind=kLoop, calls=%fused_computation.29 | loop fusion | flops 14680063 | bytes 14680064
  177.1 0.0 slice-start.1
  177.1 0.0 slice-start.2
  177.1 0.0 slice-start.3
  177.1 55.1 %fusion.12 = bf16[5,7168,512]{1,2,0:T(8,128)(2,1)} fusion(bf16[5,7168,512]{1,2,0:T(8,128)(2,1)} %fusion.16, f32[1,7168,512]{1,2,0:T(8,128)} %div.183, f32[7168]{0:T(1024)S(1)} %bitcast.67, bf16[1,7168,128]{1,2,0:T(8,128)(2,1)S(1)} %bitcast.50, bf16[1,7168,384]{1,2,0:T(8,128)(2,1)} %bitcast.44), kind=kLoop, calls=%fused_computation.24 | loop fusion | flops 44040192 | bytes 29388800
  232.2 0.0 slice-done
  232.2 0.0 slice-done.1
  232.3 0.0 slice-start.4
  232.3 0.0 slice-start.5
  232.3 0.0 slice-start.6
  232.3 0.0 slice-start.7
  232.3 55.0 %fusion.13 = bf16[5,7168,512]{1,2,0:T(8,128)(2,1)} fusion(bf16[5,7168,512]{1,2,0:T(8,128)(2,1)} %fusion.12, f32[1,7168,512]{1,2,0:T(8,128)} %div.189, f32[7168]{0:T(1024)S(1)} %bitcast.65, bf16[1,7168,128]{1,2,0:T(8,128)(2,1)S(1)} %bitcast.51, bf16[1,7168,384]{1,2,0:T(8,128)(2,1)S(1)} %bitcast.47), kind=kLoop, calls=%fused_computation.25 | loop fusion | flops 44040192 | bytes 29388800
  287.3 0.0 slice-done.2
  287.3 0.0 slice-done.3
  287.3 0.0 slice-done.4
  287.3 0.0 slice-done.5
  287.3 0.0 slice-start.8
  287.3 0.0 slice-start.9
  287.3 53.5 %fusion.14 = bf16[5,7168,512]{1,2,0:T(8,128)(2,1)} fusion(bf16[5,7168,512]{1,2,0:T(8,128)(2,1)} %fusion.13, f32[1,7168,512]{1,2,0:T(8,128)S(1)} %bitcast.55, f32[7168]{0:T(1024)S(1)} %bitcast.63, bf16[1,7168,128]{1,2,0:T(8,128)(2,1)S(1)} %bitcast.52, bf16[1,7168,384]{1,2,0:T(8,128)(2,1)S(1)} %bitcast.48), kind=kLoop, calls=%fused_computation.26 | loop fusion | flops 44040192 | bytes 29388800
  340.8 0.0 slice-done.6
  340.8 0.0 slice-done.7
  340.9 0.0 slice-done.8
  340.9 0.0 slice-done.9
  340.9 53.7 %fusion.15 = bf16[5,7168,512]{1,2,0:T(8,128)(2,1)} fusion(bf16[5,7168,512]{1,2,0:T(8,128)(2,1)} %fusion.14, f32[1,7168,512]{1,2,0:T(8,128)S(1)} %bitcast.57, f32[7168]{0:T(1024)S(1)} %bitcast.61, bf16[1,7168,128]{1,2,0:T(8,128)(2,1)S(1)} %bitcast.53, bf16[1,7168,384]{1,2,0:T(8,128)(2,1)S(1)} %bitcast.49), kind=kLoop, calls=%fused_computation.27 | loop fusion | flops 44040192 | bytes 29388800 | tf_op jit(solution)/shard_map/stack | solution.py:29
  394.6 16.9 %fusion.19 = f32[5,128,512]{1,2,0:T(8,128)S(1)} fusion(bf16[5,7168,512]{1,2,0:T(8,128)(2,1)} %fusion.15, bf16[128,7168]{1,0:T(8,128)(2,1)} %all-gather.3.cloned.1.call-done), kind=kOutput, calls=%fused_computation.34 | convolution fusion | flops 4697620480 | bytes 39845888 | tf_op jit(solution)/shard_map/tk,rkc->rtc/dot_general | solution.py:47
  411.5 0.3 fusion.24
  411.8 0.7 multiply_reduce_fusion.1
  412.5 37.0 %all-reduce = (f32[4]{0:T(128)S(1)}, f32[]{:T(128)}) all-reduce(f32[4]{0:T(128)S(1)} %fusion.24, f32[]{:T(128)} %multiply_reduce_fusion.1), channel_id=1, replica_groups=mesh['dp'=8,'mp'=4] {'dp','mp'}, use_global_device_ids=true, to_apply=%region_11.0 | all-reduce | flops 5 | bytes 40 | tf_op jit(solution)/shard_map/psum | solution.py:57
  449.5 1.3 divide_reduce_fusion
  450.8 0.7 multiply_divide_fusion
  451.4 0.7 fusion.37
  452.1 2.6 fusion.32
  454.7 0.8 copy.24
  455.5 0.7 copy.25
  456.2 0.0 copy-done
  (13 shorter events, 0.2 us)
Async XLA Ops:
  7.2 387.4 %all-gather.3.cloned.1.call-start = ((), (), s32[]{:S(2)}) async-start(), calls=%async_computation | async-start | bytes 2293760 | tf_op jit(solution)/shard_map/all_gather | solution.py:49
  171.0 61.2 %slice-start = ((s8[5505024]{0:T(1024)(128)(4,1)}), s8[1310720]{0:T(1024)(128)(4,1)S(1)}, s32[]{:S(2)}) async-start(s8[5505024]{0:T(1024)(128)(4,1)} %bitcast.45), calls=%async_computation.1 | async-start | bytes 2621440
  177.1 55.1 %slice-start.1 = ((s8[5505024]{0:T(1024)(128)(4,1)}), s8[4194304]{0:T(1024)(128)(4,1)S(1)}, s32[]{:S(2)}) async-start(s8[5505024]{0:T(1024)(128)(4,1)} %bitcast.45), calls=%async_computation.2 | async-start | bytes 8388608
  177.1 110.1 %slice-start.2 = ((s8[14680064]{0:T(1024)(128)(4,1)}), s8[4194304]{0:T(1024)(128)(4,1)S(1)}, s32[]{:S(2)}) async-start(s8[14680064]{0:T(1024)(128)(4,1)} %bitcast.54), calls=%async_computation.3 | async-start | bytes 8388608
  177.1 110.1 %slice-start.3 = ((s8[14680064]{0:T(1024)(128)(4,1)}), s8[4194304]{0:T(1024)(128)(4,1)S(1)}, s32[]{:S(2)}) async-start(s8[14680064]{0:T(1024)(128)(4,1)} %bitcast.54), calls=%async_computation.4 | async-start | bytes 8388608
  232.3 55.0 %slice-start.4 = ((s8[14680064]{0:T(1024)(128)(4,1)}), s8[4194304]{0:T(1024)(128)(4,1)S(1)}, s32[]{:S(2)}) async-start(s8[14680064]{0:T(1024)(128)(4,1)} %bitcast.54), calls=%async_computation.5 | async-start | bytes 8388608
  232.3 55.0 %slice-start.5 = ((s8[14680064]{0:T(1024)(128)(4,1)}), s8[2097152]{0:T(1024)(128)(4,1)S(1)}, s32[]{:S(2)}) async-start(s8[14680064]{0:T(1024)(128)(4,1)} %bitcast.54), calls=%async_computation.6 | async-start | bytes 4194304
  232.3 108.6 %slice-start.6 = ((s8[14680064]{0:T(1024)(128)(4,1)}), s8[4194304]{0:T(1024)(128)(4,1)S(1)}, s32[]{:S(2)}) async-start(s8[14680064]{0:T(1024)(128)(4,1)} %bitcast.56), calls=%async_computation.7 | async-start | bytes 8388608
  232.3 108.6 %slice-start.7 = ((s8[14680064]{0:T(1024)(128)(4,1)}), s8[4194304]{0:T(1024)(128)(4,1)S(1)}, s32[]{:S(2)}) async-start(s8[14680064]{0:T(1024)(128)(4,1)} %bitcast.56), calls=%async_computation.8 | async-start | bytes 8388608
  287.3 53.6 %slice-start.8 = ((s8[14680064]{0:T(1024)(128)(4,1)}), s8[4194304]{0:T(1024)(128)(4,1)S(1)}, s32[]{:S(2)}) async-start(s8[14680064]{0:T(1024)(128)(4,1)} %bitcast.56), calls=%async_computation.9 | async-start | bytes 8388608
  287.3 53.5 %slice-start.9 = ((s8[14680064]{0:T(1024)(128)(4,1)}), s8[2097152]{0:T(1024)(128)(4,1)S(1)}, s32[]{:S(2)}) async-start(s8[14680064]{0:T(1024)(128)(4,1)} %bitcast.56), calls=%async_computation.10 | async-start | bytes 4194304
  450.8 5.5 %copy-start = (f32[4]{0:T(128)}, f32[4]{0:T(128)S(1)}, u32[]{:S(2)}) copy-start(f32[4]{0:T(128)S(1)} %get-tuple-element.21) | copy-start | bytes 52
Sparse Core Ops, SparseCore 0:
  20.4 21.4 all-gather.2
where the time goes:
time: 466 us; the launch traced here: 463 us
  other arithmetic  244 us (52%)
  local copies, waits for them, and re-layouts  114 us (24%)
  blocking collectives  72.6 us (16%)
  matrix products  16.9 us (4%)
  between operations  15.6 us (3%)
    unnamed x7, other arithmetic  170 us
    div x8, local copies, waits for them, and re-layouts, fake_quant(): levels = grouped / unit_size  98.9 us
    another operation x1, other arithmetic, stack_weights(): return jnp.stack(members)  53.7 us
    psum x1, blocking collectives, per_device(): errors, energy = lax.psum((errors, energy), ('dp', 'mp'))  37 us
    psum x1, blocking collectives, per_device(): slice_sums = lax.psum(local_totals, 'dp')  21.9 us
    dot_general x1, matrix products, per_device(): jnp.einsum('tk,rkc->rtc', lax.all_gather(normed, 'mp', axis=1, tiled=True...  16.9 us
    unnamed x27, local copies, waits for them, and re-layouts  12.6 us
    reduce_max x1, other arithmetic, fake_quant(): unit_size = (jnp.max(jnp.abs(grouped), axis=1, keepdims=True) + 1e-06) / 7.0  9.52 us
  transfers between devices with their start and end apart: 1, of which 0 were waited for; matrix products, arithmetic and copies ran while one was open for 75% of the time, Pallas kernels for 0%

commit v1 on v0

v1 whole, which is shorter than its diff:
```python
import functools

import jax
import jax.numpy as jnp
from jax import lax
from jax.experimental import pallas as pl
from jax.experimental.pallas import tpu as pltpu
from jax.sharding import PartitionSpec as P

GROUP = 128
GRID = 20
RATIOS = 4
LANES = 128
BLOCK = 256
SERIES = (6.579656345395702, -12.978563343532759, 12.029937765720488, -5.563853216984216)


def swap(x, axis, distance):
    size = lax.axis_size(axis)
    return lax.ppermute(x, axis, [(i, i ^ distance) for i in range(size)])


def distances(axis):
    size = lax.axis_size(axis)
    assert size & (size - 1) == 0
    return [1 << bit for bit in range(size.bit_length() - 1)]


def total(x, axis):
    for distance in distances(axis):
        x = x + swap(x, axis, distance)
    return x


def slots(x, axis):
    blocks, order = [x], [0]
    for distance in reversed(distances(axis)):
        blocks = blocks + [swap(block, axis, distance) for block in blocks]
        order = order + [distance ^ place for place in order]
    return blocks, order


def column(row):
    return jnp.transpose(jnp.broadcast_to(row, (LANES, LANES)))


def project_kernel(order, tokens, *refs):
    count = len(order)
    me, ids, squares, live, gain = refs[:5]
    hidden = refs[5 : 5 + count]
    totals = refs[5 + count : 5 + 2 * count]
    q_ref, kv_ref = refs[5 + 2 * count : 7 + 2 * count]
    exact, approx, sums, means = refs[7 + 2 * count : 11 + 2 * count]
    normed, scales, table, stretched, shrunk, quant = refs[11 + 2 * count :]
    step = pl.program_id(0)
    rows = hidden[0].shape[0]
    width = hidden[0].shape[1]
    features = width * count
    per_slot = width // LANES

    @pl.when(step == 0)
    def _():
        for slot in range(count):
            owner = me[0] ^ order[slot]
            for piece in range(per_slot):
                means[pl.ds(owner * per_slot + piece, 1), :] = totals[slot][piece : piece + 1, :]
        sums_all = means[...]
        logged = jnp.log(sums_all + 1e-06)
        centred = logged - 0.5 * (jnp.max(logged) + jnp.min(logged))
        means[...] = sums_all / tokens
        for ratio in range(RATIOS):
            alpha = ids[ratio].astype(jnp.float32) / GRID
            scale = jnp.exp(alpha * centred)
            scales[:, ratio, :] = scale
            scales[:, RATIOS + ratio, :] = 1.0 / scale
        for top in range(0, rows, LANES):
            mean_square = squares[:, top : top + LANES] / features
            rooted = column(lax.rsqrt(mean_square + 1e-06))
            for slot in range(count):
                owner = me[0] ^ order[slot]
                for piece in range(per_slot):
                    place = owner * per_slot + piece
                    values = hidden[slot][top : top + LANES, piece * LANES : (piece + 1) * LANES]
                    values = values.astype(jnp.float32) * rooted * gain[pl.ds(place, 1), :]
                    normed[place, top : top + LANES, :] = values.astype(jnp.bfloat16)
        exact[...] = jnp.zeros_like(exact)
        approx[...] = jnp.zeros_like(approx)

    groups = BLOCK // GROUP
    parts = [(q_ref, at) for at in range(0, q_ref.shape[1], LANES)]
    parts += [(kv_ref, at) for at in range(0, kv_ref.shape[1], LANES)]
    for group in range(groups):
        table[...] = jnp.transpose(scales[step * groups + group])
        for ratio in range(RATIOS):
            stretched[ratio] = jnp.broadcast_to(table[:, ratio : ratio + 1], (LANES, LANES))
            shrunk[ratio] = jnp.broadcast_to(
                table[:, RATIOS + ratio : RATIOS + ratio + 1], (LANES, LANES)
            ).astype(jnp.bfloat16)
        for spot, (ref, at) in enumerate(parts):
            weight = ref[group * GROUP : (group + 1) * GROUP, at : at + LANES]
            wide = weight.astype(jnp.float32)
            for ratio in range(RATIOS):
                scaled = wide * stretched[ratio]
                peak = jnp.max(jnp.abs(scaled), axis=0, keepdims=True)
                unit = (peak + 1e-06) / 7.0
                level = scaled * (1.0 / unit)
                part = (level - jnp.round(level)).astype(jnp.bfloat16)
                square = part * part
                series = jnp.full_like(square, SERIES[-1])
                for term in SERIES[-2::-1]:
                    series = series * square + jnp.bfloat16(term)
                wave = part - part * square * series
                wave = wave * unit.astype(jnp.bfloat16) * shrunk[ratio]
                quant[ratio, group * GROUP : (group + 1) * GROUP, spot * LANES : (spot + 1) * LANES] = weight - wave
    left = jnp.concatenate([normed[step * groups + group] for group in range(groups)], axis=1)
    for ratio in range(RATIOS):
        approx[ratio] += jnp.dot(left, quant[ratio], preferred_element_type=jnp.float32)
    query = q_ref.shape[1]
    exact[:, :query] += jnp.dot(left, q_ref[...], preferred_element_type=jnp.float32)
    exact[:, query:] += jnp.dot(left, kv_ref[...], preferred_element_type=jnp.float32)

    @pl.when(step == pl.num_programs(0) - 1)
    def _():
        masks = [column(live[:, top : top + LANES].astype(jnp.float32)) for top in range(0, rows, LANES)]
        for ratio in range(RATIOS + 1):
            gathered = jnp.zeros((1, LANES), jnp.float32)
            for index, top in enumerate(range(0, rows, LANES)):
                for at in range(0, exact.shape[1], LANES):
                    value = exact[top : top + LANES, at : at + LANES]
                    if ratio < RATIOS:
                        value = approx[ratio, top : top + LANES, at : at + LANES] - value
                    value = value * masks[index]
                    gathered = gathered + jnp.sum(value * value, axis=0, keepdims=True)
            sums[ratio : ratio + 1, :] = gathered
        sums[RATIOS + 1 :, :] = jnp.zeros((8 - RATIOS - 1, LANES), jnp.float32)


def blend_kernel(sums, approx, losses, query, kv):
    folded = [jnp.sum(sums[ratio : ratio + 1, :], axis=1, keepdims=True) for ratio in range(RATIOS + 1)]
    loss = [folded[ratio] / folded[RATIOS] for ratio in range(RATIOS)]
    inverse = [1.0 / (value * value) for value in loss]
    whole = inverse[0] + inverse[1] + inverse[2] + inverse[3]
    for ratio in range(RATIOS):
        losses[ratio : ratio + 1, :] = jnp.broadcast_to(loss[ratio], (1, LANES))
    blended = (inverse[0] / whole) * approx[0]
    for ratio in range(1, RATIOS):
        blended = blended + (inverse[ratio] / whole) * approx[ratio]
    blended = blended.astype(jnp.bfloat16)
    query[...] = blended[:, : query.shape[1]]
    kv[...] = blended[:, query.shape[1] :]


def per_device(hidden, live, norm_gain, q_weight, kv_weight, ratio_ids):
    rows, width = hidden.shape
    shards = lax.axis_size("mp")
    features = width * shards
    tokens = rows * lax.axis_size("dp")
    query, kv = q_weight.shape[1], kv_weight.shape[1]
    me = lax.axis_index("mp")

    values = hidden.astype(jnp.float32)
    squares = total(jnp.sum(values * values, axis=1).reshape(1, rows), "mp")
    gain_slice = lax.dynamic_slice_in_dim(norm_gain, me * width, width)
    scaling = lax.rsqrt(squares.reshape(rows, 1) / features + 1e-06)
    own = (values * scaling * gain_slice[None, :]).astype(jnp.bfloat16)
    live_rows = live.astype(jnp.float32)[:, None]
    sums = jnp.sum(jnp.abs(own.astype(jnp.float32)) * live_rows, axis=0)
    sums = total(sums.reshape(width // LANES, LANES), "dp")
    total_slots, order = slots(sums, "mp")
    hidden_slots, _ = slots(hidden, "mp")

    whole = lambda shape: pl.BlockSpec(shape, lambda i: (0,) * len(shape))
    scalar = pl.BlockSpec(memory_space=pltpu.SMEM)
    exact, approx, sums, means = pl.pallas_call(
        functools.partial(project_kernel, tuple(order), float(tokens)),
        grid=(features // BLOCK,),
        in_specs=[scalar, scalar, whole((1, rows)), whole((1, rows)), whole((features // LANES, LANES))]
        + [whole((rows, width))] * shards
        + [whole((width // LANES, LANES))] * shards
        + [
            pl.BlockSpec((BLOCK, query), lambda i: (i, 0)),
            pl.BlockSpec((BLOCK, kv), lambda i: (i, 0)),
        ],
        out_specs=[
            whole((rows, query + kv)),
            whole((RATIOS, rows, query + kv)),
            whole((8, LANES)),
            whole((features // LANES, LANES)),
        ],
        out_shape=[
            jax.ShapeDtypeStruct((rows, query + kv), jnp.float32),
            jax.ShapeDtypeStruct((RATIOS, rows, query + kv), jnp.float32),
            jax.ShapeDtypeStruct((8, LANES), jnp.float32),
            jax.ShapeDtypeStruct((features // LANES, LANES), jnp.float32),
        ],
        scratch_shapes=[
            pltpu.VMEM((features // LANES, rows, LANES), jnp.bfloat16),
            pltpu.VMEM((features // LANES, 8, LANES), jnp.float32),
            pltpu.VMEM((LANES, 8), jnp.float32),
            pltpu.VMEM((RATIOS, LANES, LANES), jnp.float32),
            pltpu.VMEM((RATIOS, LANES, LANES), jnp.bfloat16),
            pltpu.VMEM((RATIOS, BLOCK, query + kv), jnp.bfloat16),
        ],
        name="project",
    )(
        me.reshape(1).astype(jnp.int32),
        ratio_ids,
        squares,
        live.reshape(1, rows),
        norm_gain.reshape(features // LANES, LANES),
        *hidden_slots,
        *total_slots,
        q_weight,
        kv_weight,
    )
    sums = total(total(sums, "mp"), "dp")
    losses, q_latent, kv_latent = pl.pallas_call(
        blend_kernel,
        out_shape=[
            jax.ShapeDtypeStruct((RATIOS, LANES), jnp.float32),
            jax.ShapeDtypeStruct((rows, query), jnp.bfloat16),
            jax.ShapeDtypeStruct((rows, kv), jnp.bfloat16),
        ],
        name="blend",
    )(sums, approx)
    return losses[:, 0], q_latent, kv_latent, means.reshape(features)


def solution(mesh):
    placed = (P("dp", "mp"), P("dp"), P(), P(None, "mp"), P(None, "mp"), P())
    return jax.shard_map(
        per_device,
        mesh=mesh,
        in_specs=placed,
        out_specs=(P(), P("dp", "mp"), P("dp", "mp"), P()),
        check_vma=False,
    )
```

time: 466 us -> 110 us (0.24)
  other arithmetic: 244 us -> 4.93 us
  local copies, waits for them, and re-layouts: 114 us -> 2.98 us
  blocking collectives: 72.6 us -> 0 us
  Pallas kernels: 0 us -> 54.8 us
  waiting for transfers between devices: 0.02 us -> 25.2 us
  starting transfers between devices: 0.04 us -> 21.4 us
  matrix products: 16.9 us -> 0 us
  between operations: 15.6 us -> 0.73 us
    unnamed x7 -> x0, other arithmetic: 170 us -> none
    div x12 -> x0, local copies, waits for them, and re-layouts: 99.3 us -> none  [the longest x8 98.9 us: fake_quant(): levels = grouped / unit_size]
    psum x3 -> x0, blocking collectives: 67.3 us -> none  [the longest x1 37 us: per_device(): errors, energy = lax.psum((errors, energy), ('dp', 'mp'))]
    pallas_call x0 -> x2, Pallas kernels: none -> 54.8 us  [the longest x1 52.7 us: per_device(): pl.pallas_call(functools.partial(project_kernel, tuple(order), float(toke...]
    another operation x1 -> x0, other arithmetic: 53.7 us -> none  [stack_weights(): return jnp.stack(members)]
    ppermute x0 -> x16, waiting for transfers between devices: none -> 25.2 us  [swap(): return lax.ppermute(x, axis, [(i, i ^ distance) for i in range(size)])]
    ppermute x0 -> x16, starting transfers between devices: none -> 21.4 us  [swap(): return lax.ppermute(x, axis, [(i, i ^ distance) for i in range(size)])]
    dot_general x1 -> x0, matrix products: 16.9 us -> none  [per_device(): jnp.einsum('tk,rkc->rtc', lax.all_gather(normed, 'mp', axis=1, tiled=True...]
  transfers between devices with their start and end apart: 1 -> 16, of which waited for: 0 -> 11; matrix products, arithmetic and copies ran while one was open for 75% -> 3% of each run, Pallas kernels for 0% -> 0%
where the time goes in v1:
time: 110 us
  Pallas kernels  54.8 us (50%)
  waiting for transfers between devices  25.2 us (23%)
  starting transfers between devices  21.4 us (19%)
  other arithmetic  4.93 us (4%)
  local copies, waits for them, and re-layouts  2.98 us (3%)
    pallas_call x1, Pallas kernels, per_device(): pl.pallas_call(functools.partial(project_kernel, tuple(order), float(toke...  52.7 us
    ppermute x16, waiting for transfers between devices, swap(): return lax.ppermute(x, axis, [(i, i ^ distance) for i in range(size)])  25.2 us
    ppermute x16, starting transfers between devices, swap(): return lax.ppermute(x, axis, [(i, i ^ distance) for i in range(size)])  21.4 us
  transfers between devices with their start and end apart: 16, of which 11 were waited for; matrix products, arithmetic and copies ran while one was open for 3% of the time, Pallas kernels for 0%

profile of v1, /device:TPU:0, one launch (start us, length us, event | category | flops | bytes accessed | tf_op | source)
XLA Modules:
  0.0 110.0 jit_solution(15649762237858125678)
XLA Ops:
  0.6 1.2 %fusion = f32[128]{0:T(128)S(1)} fusion(bf16[128,1792]{1,0:T(8,128)(2,1)} %refs_5_.1), kind=kLoop, calls=%fused_computation.2 | loop fusion | flops 688000 | bytes 459264 | tf_op jit(solution)/shard_map/reduce_sum | solution.py:162
  1.8 0.6 collective-permute-start
  2.4 2.6 %collective-permute-start.2 = (bf16[128,1792]{1,0:T(8,128)(2,1)}, bf16[128,1792]{1,0:T(8,128)(2,1)S(1)}, u32[]{:S(2)}, u32[]{:S(2)}) collective-permute-start(bf16[128,1792]{1,0:T(8,128)(2,1)} %refs_5_.1), channel_id=1, source_target_pairs={{0,2},{1,3},{2,0},{3,1},{4,6},{5,7},{6,4},{7,5},{8,10},{9,11},{10,... | collective-permute-start | bytes 1376264 | tf_op jit(solution)/shard_map/ppermute | solution.py:20
  4.9 0.0 collective-permute-done
  4.9 1.1 collective-permute-start.1
  6.0 0.7 convert_element_type.15
  6.7 0.8 dynamic_slice.3
  7.5 8.9 %collective-permute-done.1 = f32[1,128]{1,0:T(1,128)S(1)} collective-permute-done((f32[1,128]{1,0:T(1,128)S(1)}, f32[1,128]{1,0:T(1,128)S(1)}, u32[]{:S(2)}, u32[]{:S(2)}) %collective-permute-start.1) | collective-permute-done | bytes 544 | tf_op jit(solution)/shard_map/ppermute | solution.py:20
  16.3 0.5 rsqrt_bitcast_fusion
  16.9 1.3 %multiply_reduce_fusion = f32[1792]{0:T(1024)S(1)} fusion(bf16[128,1792]{1,0:T(8,128)(2,1)} %refs_5_.1, f32[128]{0:T(128)S(1)} %convert_element_type.15, f32[1792]{0:T(1024)S(1)} %dynamic_slice.3, f32[128]{0:T(128)S(1)} %get-tuple-element.16), kind=kLoop, calls=%fused_computation.5 | loop fusion | flops 1833216 | bytes 474112 | tf_op jit(solution)/shard_map/reduce_sum | solution.py:167
  18.2 1.8 %collective-permute-start.5 = (f32[14,128]{1,0:T(8,128)S(1)}, f32[14,128]{1,0:T(8,128)S(1)}, u32[]{:S(2)}, u32[]{:S(2)}) collective-permute-start(f32[14,128]{1,0:T(8,128)S(1)} %bitcast.12), channel_id=1, source_target_pairs={{0,4},{4,0},{8,12},{12,8},{16,20},{20,16},{24,28},{28,24},{1,5},{5... | collective-permute-start | bytes 21512 | tf_op jit(solution)/shard_map/ppermute | solution.py:20
  20.0 0.0 collective-permute-start.3
  20.0 0.0 collective-permute-done.2.refs_6_
  20.0 0.0 copy-start
  20.0 0.5 collective-permute-start.4
  20.5 1.4 %collective-permute-done.5 = f32[14,128]{1,0:T(8,128)S(1)} collective-permute-done((f32[14,128]{1,0:T(8,128)S(1)}, f32[14,128]{1,0:T(8,128)S(1)}, u32[]{:S(2)}, u32[]{:S(2)}) %collective-permute-start.5) | collective-permute-done | bytes 7200 | tf_op jit(solution)/shard_map/ppermute | solution.py:20
  21.9 1.8 %collective-permute-start.6 = (f32[14,128]{1,0:T(8,128)S(1)}, f32[14,128]{1,0:T(8,128)S(1)}, u32[]{:S(2)}, u32[]{:S(2)}) collective-permute-start(f32[14,128]{1,0:T(8,128)S(1)} %bitcast_add_fusion), channel_id=1, source_target_pairs={{0,8},{4,12},{8,0},{12,4},{16,24},{20,28},{24,16},{28,20},{1,9},{5... | collective-permute-start | bytes 21512 | tf_op jit(solution)/shard_map/ppermute | solution.py:20
  23.7 1.8 %collective-permute-done.6 = f32[14,128]{1,0:T(8,128)S(1)} collective-permute-done((f32[14,128]{1,0:T(8,128)S(1)}, f32[14,128]{1,0:T(8,128)S(1)}, u32[]{:S(2)}, u32[]{:S(2)}) %collective-permute-start.6) | collective-permute-done | bytes 7200 | tf_op jit(solution)/shard_map/ppermute | solution.py:20
  25.5 2.8 %collective-permute-start.7 = (f32[14,128]{1,0:T(8,128)S(1)}, f32[14,128]{1,0:T(8,128)S(1)}, u32[]{:S(2)}, u32[]{:S(2)}) collective-permute-start(f32[14,128]{1,0:T(8,128)S(1)} %fusion.3), channel_id=1, source_target_pairs={{0,16},{4,20},{8,24},{12,28},{16,0},{20,4},{24,8},{28,12},{1,17},{... | collective-permute-start | bytes 21512 | tf_op jit(solution)/shard_map/ppermute | solution.py:20
  28.4 1.7 %collective-permute-done.7 = f32[14,128]{1,0:T(8,128)S(1)} collective-permute-done((f32[14,128]{1,0:T(8,128)S(1)}, f32[14,128]{1,0:T(8,128)S(1)}, u32[]{:S(2)}, u32[]{:S(2)}) %collective-permute-start.7) | collective-permute-done | bytes 7200 | tf_op jit(solution)/shard_map/ppermute | solution.py:20
  30.1 0.0 copy-start.3
  30.1 1.7 %collective-permute-start.8 = (f32[14,128]{1,0:T(8,128)S(1)}, f32[14,128]{1,0:T(8,128)S(1)}, u32[]{:S(2)}, u32[]{:S(2)}) collective-permute-start(f32[14,128]{1,0:T(8,128)S(1)} %add.52.refs_9_), channel_id=1, source_target_pairs={{0,2},{1,3},{2,0},{3,1},{4,6},{5,7},{6,4},{7,5},{8,10},{9,11},{10,... | collective-permute-start | bytes 21512 | tf_op jit(solution)/shard_map/ppermute | solution.py:20
  31.8 0.0 collective-permute-start.9
  31.8 1.9 %collective-permute-done.8.refs_10_ = f32[14,128]{1,0:T(8,128)S(1)} collective-permute-done((f32[14,128]{1,0:T(8,128)S(1)}, f32[14,128]{1,0:T(8,128)S(1)}, u32[]{:S(2)}, u32[]{:S(2)}) %collective-permute-start.8) | collective-permute-done | bytes 7200 | tf_op jit(solution)/shard_map/ppermute | solution.py:20
  33.7 0.0 copy-start.4
  33.7 0.0 collective-permute-start.10
  33.7 0.0 collective-permute-done.9.refs_11_
  33.7 0.0 copy-start.5
  33.8 1.2 %collective-permute-done.10.refs_12_ = f32[14,128]{1,0:T(8,128)S(1)} collective-permute-done((f32[14,128]{1,0:T(8,128)S(1)}, f32[14,128]{1,0:T(8,128)S(1)}, u32[]{:S(2)}, u32[]{:S(2)}) %collective-permute-start.10) | collective-permute-done | bytes 7200 | tf_op jit(solution)/shard_map/ppermute | solution.py:20
  34.9 0.0 copy-start.6
  34.9 0.0 collective-permute-done.3.refs_7_
  34.9 0.0 copy-start.1
  34.9 0.0 collective-permute-done.4.refs_8_
  34.9 0.0 copy-start.2
  34.9 0.0 copy-done
  34.9 0.0 copy-done.3
  35.0 0.0 copy-done.4
  35.0 0.0 copy-done.5
  35.0 0.5 copy-done.6
  35.5 0.2 copy-done.1
  35.7 0.2 copy-done.2
  35.8 52.7 %project.1 = (f32[128,512]{1,0:T(8,128)}, f32[4,128,512]{2,1,0:T(8,128)}, f32[8,128]{1,0:T(8,128)}, f32[56,128]{1,0:T(8,128)}) custom-call(s32[1]{0:T(128)} %bitcast.refs_0_, s32[4]{0:T(128)} %refs_1_.1, f32[1,128]{1,0:T(1,128)} %get-tuple-element.17.refs_2_, s32[1,128]{1,0:T(1,128)} %bitcast.14, f32[56,128]{1,0:T(8,128)} %bitcast.13, ...), custom_call_target="tpu_custom_call" | custom-call | tf_op jit(solution)/shard_map/project/pallas_call | solution.py:174
  88.6 0.2 collective-permute-start.11
  88.8 1.2 %collective-permute-done.11 = f32[8,128]{1,0:T(8,128)S(1)} collective-permute-done((f32[8,128]{1,0:T(8,128)}, f32[8,128]{1,0:T(8,128)S(1)}, u32[]{:S(2)}, u32[]{:S(2)}) %collective-permute-start.11) | collective-permute-done | bytes 4128 | tf_op jit(solution)/shard_map/ppermute | solution.py:20
  90.0 0.7 add.53
  90.7 1.7 %collective-permute-start.12 = (f32[8,128]{1,0:T(8,128)S(1)}, f32[8,128]{1,0:T(8,128)S(1)}, u32[]{:S(2)}, u32[]{:S(2)}) collective-permute-start(f32[8,128]{1,0:T(8,128)S(1)} %add.53), channel_id=1, source_target_pairs={{0,2},{1,3},{2,0},{3,1},{4,6},{5,7},{6,4},{7,5},{8,10},{9,11},{10,... | collective-permute-start | bytes 12296 | tf_op jit(solution)/shard_map/ppermute | solution.py:20
  92.4 1.9 %collective-permute-done.12 = f32[8,128]{1,0:T(8,128)S(1)} collective-permute-done((f32[8,128]{1,0:T(8,128)S(1)}, f32[8,128]{1,0:T(8,128)S(1)}, u32[]{:S(2)}, u32[]{:S(2)}) %collective-permute-start.12) | collective-permute-done | bytes 4128 | tf_op jit(solution)/shard_map/ppermute | solution.py:20
  94.3 1.8 %collective-permute-start.13 = (f32[8,128]{1,0:T(8,128)S(1)}, f32[8,128]{1,0:T(8,128)S(1)}, u32[]{:S(2)}, u32[]{:S(2)}) collective-permute-start(f32[8,128]{1,0:T(8,128)S(1)} %add.54), channel_id=1, source_target_pairs={{0,4},{4,0},{8,12},{12,8},{16,20},{20,16},{24,28},{28,24},{1,5},{5... | collective-permute-start | bytes 12296 | tf_op jit(solution)/shard_map/ppermute | solution.py:20
  96.1 1.8 %collective-permute-done.13 = f32[8,128]{1,0:T(8,128)S(1)} collective-permute-done((f32[8,128]{1,0:T(8,128)S(1)}, f32[8,128]{1,0:T(8,128)S(1)}, u32[]{:S(2)}, u32[]{:S(2)}) %collective-permute-start.13) | collective-permute-done | bytes 4128 | tf_op jit(solution)/shard_map/ppermute | solution.py:20
  97.9 1.8 %collective-permute-start.14 = (f32[8,128]{1,0:T(8,128)S(1)}, f32[8,128]{1,0:T(8,128)S(1)}, u32[]{:S(2)}, u32[]{:S(2)}) collective-permute-start(f32[8,128]{1,0:T(8,128)S(1)} %add.55), channel_id=1, source_target_pairs={{0,8},{4,12},{8,0},{12,4},{16,24},{20,28},{24,16},{28,20},{1,9},{5... | collective-permute-start | bytes 12296 | tf_op jit(solution)/shard_map/ppermute | solution.py:20
  99.7 1.8 %collective-permute-done.14 = f32[8,128]{1,0:T(8,128)S(1)} collective-permute-done((f32[8,128]{1,0:T(8,128)S(1)}, f32[8,128]{1,0:T(8,128)S(1)}, u32[]{:S(2)}, u32[]{:S(2)}) %collective-permute-start.14) | collective-permute-done | bytes 4128 | tf_op jit(solution)/shard_map/ppermute | solution.py:20
  101.5 2.8 %collective-permute-start.15 = (f32[8,128]{1,0:T(8,128)S(1)}, f32[8,128]{1,0:T(8,128)S(1)}, u32[]{:S(2)}, u32[]{:S(2)}) collective-permute-start(f32[8,128]{1,0:T(8,128)S(1)} %add.56), channel_id=1, source_target_pairs={{0,16},{4,20},{8,24},{12,28},{16,0},{20,4},{24,8},{28,12},{1,17},{... | collective-permute-start | bytes 12296 | tf_op jit(solution)/shard_map/ppermute | solution.py:20
  104.4 1.7 %collective-permute-done.15 = f32[8,128]{1,0:T(8,128)S(1)} collective-permute-done((f32[8,128]{1,0:T(8,128)S(1)}, f32[8,128]{1,0:T(8,128)S(1)}, u32[]{:S(2)}, u32[]{:S(2)}) %collective-permute-start.15) | collective-permute-done | bytes 4128 | tf_op jit(solution)/shard_map/ppermute | solution.py:20
  106.0 0.6 add.57.sums
  106.6 2.1 %blend.1 = (f32[4,128]{1,0:T(4,128)}, bf16[128,384]{1,0:T(8,128)(2,1)}, bf16[128,128]{1,0:T(8,128)(2,1)}) custom-call(f32[8,128]{1,0:T(8,128)} %add.57.sums, f32[4,128,512]{2,1,0:T(8,128)} %get-tuple-element.11.approx), custom_call_target="tpu_custom_call" | custom-call | tf_op jit(solution)/shard_map/blend/pallas_call | solution.py:217
  108.7 1.3 %slice_reduce_fusion = f32[4]{0:T(128)} fusion(f32[4,128]{1,0:T(4,128)} %get-tuple-element.12), kind=kLoop, calls=%fused_computation.6 | loop fusion | bytes 32 | tf_op jit(solution)/shard_map/slice | solution.py:226
  (7 shorter events, 0.0 us)
Async XLA Ops:
  1.8 3.1 %collective-permute-start = (f32[1,128]{1,0:T(1,128)S(1)}, f32[1,128]{1,0:T(1,128)S(1)}, u32[]{:S(2)}, u32[]{:S(2)}) collective-permute-start(f32[1,128]{1,0:T(1,128)S(1)} %bitcast.15), channel_id=1, source_target_pairs={{0,1},{1,0},{2,3},{3,2},{4,5},{5,4},{6,7},{7,6},{8,9},{9,8},{10,11... | collective-permute-start | bytes 1544 | tf_op jit(solution)/shard_map/ppermute | solution.py:20
  2.4 17.6 %collective-permute-start.2 = (bf16[128,1792]{1,0:T(8,128)(2,1)}, bf16[128,1792]{1,0:T(8,128)(2,1)S(1)}, u32[]{:S(2)}, u32[]{:S(2)}) collective-permute-start(bf16[128,1792]{1,0:T(8,128)(2,1)} %refs_5_.1), channel_id=1, source_target_pairs={{0,2},{1,3},{2,0},{3,1},{4,6},{5,7},{6,4},{7,5},{8,10},{9,11},{10,... | collective-permute-start | bytes 1376264 | tf_op jit(solution)/shard_map/ppermute | solution.py:20
  4.9 11.4 %collective-permute-start.1 = (f32[1,128]{1,0:T(1,128)S(1)}, f32[1,128]{1,0:T(1,128)S(1)}, u32[]{:S(2)}, u32[]{:S(2)}) collective-permute-start(f32[1,128]{1,0:T(1,128)S(1)} %bitcast_add_fusion.1), channel_id=1, source_target_pairs={{0,2},{1,3},{2,0},{3,1},{4,6},{5,7},{6,4},{7,5},{8,10},{9,11},{10,... | collective-permute-start | bytes 1544 | tf_op jit(solution)/shard_map/ppermute | solution.py:20
  18.2 3.7 %collective-permute-start.5 = (f32[14,128]{1,0:T(8,128)S(1)}, f32[14,128]{1,0:T(8,128)S(1)}, u32[]{:S(2)}, u32[]{:S(2)}) collective-permute-start(f32[14,128]{1,0:T(8,128)S(1)} %bitcast.12), channel_id=1, source_target_pairs={{0,4},{4,0},{8,12},{12,8},{16,20},{20,16},{24,28},{28,24},{1,5},{5... | collective-permute-start | bytes 21512 | tf_op jit(solution)/shard_map/ppermute | solution.py:20
  20.0 14.9 %collective-permute-start.3 = (bf16[128,1792]{1,0:T(8,128)(2,1)}, bf16[128,1792]{1,0:T(8,128)(2,1)S(1)}, u32[]{:S(2)}, u32[]{:S(2)}) collective-permute-start(bf16[128,1792]{1,0:T(8,128)(2,1)} %refs_5_.1), channel_id=1, source_target_pairs={{0,1},{1,0},{2,3},{3,2},{4,5},{5,4},{6,7},{7,6},{8,9},{9,8},{10,11... | collective-permute-start | bytes 1376264 | tf_op jit(solution)/shard_map/ppermute | solution.py:20
  20.0 14.9 %copy-start = (bf16[128,1792]{1,0:T(8,128)(2,1)}, bf16[128,1792]{1,0:T(8,128)(2,1)S(1)}, u32[]{:S(2)}) copy-start(bf16[128,1792]{1,0:T(8,128)(2,1)S(1)} %collective-permute-done.2.refs_6_) | copy-start | bytes 1376260
  20.0 14.9 %collective-permute-start.4 = (bf16[128,1792]{1,0:T(8,128)(2,1)S(1)}, bf16[128,1792]{1,0:T(8,128)(2,1)S(1)}, u32[]{:S(2)}, u32[]{:S(2)}) collective-permute-start(bf16[128,1792]{1,0:T(8,128)(2,1)S(1)} %collective-permute-done.2.refs_6_), channel_id=1, source_target_pairs={{0,1},{1,0},{2,3},{3,2},{4,5},{5,4},{6,7},{7,6},{8,9},{9,8},{10,11... | collective-permute-start | bytes 1376264 | tf_op jit(solution)/shard_map/ppermute | solution.py:20
  21.9 3.7 %collective-permute-start.6 = (f32[14,128]{1,0:T(8,128)S(1)}, f32[14,128]{1,0:T(8,128)S(1)}, u32[]{:S(2)}, u32[]{:S(2)}) collective-permute-start(f32[14,128]{1,0:T(8,128)S(1)} %bitcast_add_fusion), channel_id=1, source_target_pairs={{0,8},{4,12},{8,0},{12,4},{16,24},{20,28},{24,16},{28,20},{1,9},{5... | collective-permute-start | bytes 21512 | tf_op jit(solution)/shard_map/ppermute | solution.py:20
  25.5 4.5 %collective-permute-start.7 = (f32[14,128]{1,0:T(8,128)S(1)}, f32[14,128]{1,0:T(8,128)S(1)}, u32[]{:S(2)}, u32[]{:S(2)}) collective-permute-start(f32[14,128]{1,0:T(8,128)S(1)} %fusion.3), channel_id=1, source_target_pairs={{0,16},{4,20},{8,24},{12,28},{16,0},{20,4},{24,8},{28,12},{1,17},{... | collective-permute-start | bytes 21512 | tf_op jit(solution)/shard_map/ppermute | solution.py:20
  30.1 4.9 %copy-start.3 = (f32[14,128]{1,0:T(8,128)}, f32[14,128]{1,0:T(8,128)S(1)}, u32[]{:S(2)}) copy-start(f32[14,128]{1,0:T(8,128)S(1)} %add.52.refs_9_) | copy-start | bytes 21508
  30.1 3.7 %collective-permute-start.8 = (f32[14,128]{1,0:T(8,128)S(1)}, f32[14,128]{1,0:T(8,128)S(1)}, u32[]{:S(2)}, u32[]{:S(2)}) collective-permute-start(f32[14,128]{1,0:T(8,128)S(1)} %add.52.refs_9_), channel_id=1, source_target_pairs={{0,2},{1,3},{2,0},{3,1},{4,6},{5,7},{6,4},{7,5},{8,10},{9,11},{10,... | collective-permute-start | bytes 21512 | tf_op jit(solution)/shard_map/ppermute | solution.py:20
  31.8 1.9 %collective-permute-start.9 = (f32[14,128]{1,0:T(8,128)S(1)}, f32[14,128]{1,0:T(8,128)S(1)}, u32[]{:S(2)}, u32[]{:S(2)}) collective-permute-start(f32[14,128]{1,0:T(8,128)S(1)} %add.52.refs_9_), channel_id=1, source_target_pairs={{0,1},{1,0},{2,3},{3,2},{4,5},{5,4},{6,7},{7,6},{8,9},{9,8},{10,11... | collective-permute-start | bytes 21512 | tf_op jit(solution)/shard_map/ppermute | solution.py:20
  33.7 1.2 %copy-start.4 = (f32[14,128]{1,0:T(8,128)}, f32[14,128]{1,0:T(8,128)S(1)}, u32[]{:S(2)}) copy-start(f32[14,128]{1,0:T(8,128)S(1)} %collective-permute-done.8.refs_10_) | copy-start | bytes 21508
  33.7 1.2 %collective-permute-start.10 = (f32[14,128]{1,0:T(8,128)S(1)}, f32[14,128]{1,0:T(8,128)S(1)}, u32[]{:S(2)}, u32[]{:S(2)}) collective-permute-start(f32[14,128]{1,0:T(8,128)S(1)} %collective-permute-done.8.refs_10_), channel_id=1, source_target_pairs={{0,1},{1,0},{2,3},{3,2},{4,5},{5,4},{6,7},{7,6},{8,9},{9,8},{10,11... | collective-permute-start | bytes 21512 | tf_op jit(solution)/shard_map/ppermute | solution.py:20
  33.7 1.2 %copy-start.5 = (f32[14,128]{1,0:T(8,128)}, f32[14,128]{1,0:T(8,128)S(1)}, u32[]{:S(2)}) copy-start(f32[14,128]{1,0:T(8,128)S(1)} %collective-permute-done.9.refs_11_) | copy-start | bytes 21508
  34.9 0.6 copy-start.6
  34.9 0.8 copy-start.1
  34.9 0.9 copy-start.2
  88.6 1.4 %collective-permute-start.11 = (f32[8,128]{1,0:T(8,128)}, f32[8,128]{1,0:T(8,128)S(1)}, u32[]{:S(2)}, u32[]{:S(2)}) collective-permute-start(f32[8,128]{1,0:T(8,128)} %get-tuple-element.10), channel_id=1, source_target_pairs={{0,1},{1,0},{2,3},{3,2},{4,5},{5,4},{6,7},{7,6},{8,9},{9,8},{10,11... | collective-permute-start | bytes 12296 | tf_op jit(solution)/shard_map/ppermute | solution.py:20
  90.7 3.6 %collective-permute-start.12 = (f32[8,128]{1,0:T(8,128)S(1)}, f32[8,128]{1,0:T(8,128)S(1)}, u32[]{:S(2)}, u32[]{:S(2)}) collective-permute-start(f32[8,128]{1,0:T(8,128)S(1)} %add.53), channel_id=1, source_target_pairs={{0,2},{1,3},{2,0},{3,1},{4,6},{5,7},{6,4},{7,5},{8,10},{9,11},{10,... | collective-permute-start | bytes 12296 | tf_op jit(solution)/shard_map/ppermute | solution.py:20
  94.3 3.6 %collective-permute-start.13 = (f32[8,128]{1,0:T(8,128)S(1)}, f32[8,128]{1,0:T(8,128)S(1)}, u32[]{:S(2)}, u32[]{:S(2)}) collective-permute-start(f32[8,128]{1,0:T(8,128)S(1)} %add.54), channel_id=1, source_target_pairs={{0,4},{4,0},{8,12},{12,8},{16,20},{20,16},{24,28},{28,24},{1,5},{5... | collective-permute-start | bytes 12296 | tf_op jit(solution)/shard_map/ppermute | solution.py:20
  97.9 3.6 %collective-permute-start.14 = (f32[8,128]{1,0:T(8,128)S(1)}, f32[8,128]{1,0:T(8,128)S(1)}, u32[]{:S(2)}, u32[]{:S(2)}) collective-permute-start(f32[8,128]{1,0:T(8,128)S(1)} %add.55), channel_id=1, source_target_pairs={{0,8},{4,12},{8,0},{12,4},{16,24},{20,28},{24,16},{28,20},{1,9},{5... | collective-permute-start | bytes 12296 | tf_op jit(solution)/shard_map/ppermute | solution.py:20
  101.5 4.5 %collective-permute-start.15 = (f32[8,128]{1,0:T(8,128)S(1)}, f32[8,128]{1,0:T(8,128)S(1)}, u32[]{:S(2)}, u32[]{:S(2)}) collective-permute-start(f32[8,128]{1,0:T(8,128)S(1)} %add.56), channel_id=1, source_target_pairs={{0,16},{4,20},{8,24},{12,28},{16,0},{20,4},{24,8},{28,12},{1,17},{... | collective-permute-start | bytes 12296 | tf_op jit(solution)/shard_map/ppermute | solution.py:20

commit v2 on v1

v2 whole, which is shorter than its diff:
```python
import functools

import jax
import jax.numpy as jnp
from jax import lax
from jax.experimental import pallas as pl
from jax.experimental.pallas import tpu as pltpu
from jax.sharding import PartitionSpec as P

GROUP = 128
GRID = 20
RATIOS = 4
LANES = 128
HALF = 256
LINEAR, CONSTANT, GAIN = -1.1640625, 0.458984375, 8.705


def swap(x, axis, distance):
    size = lax.axis_size(axis)
    return lax.ppermute(x, axis, [(i, i ^ distance) for i in range(size)])


def distances(axis):
    size = lax.axis_size(axis)
    assert size & (size - 1) == 0
    return [1 << bit for bit in range(size.bit_length() - 1)]


def total(x, axis):
    for distance in distances(axis):
        x = x + swap(x, axis, distance)
    return x


def peers(x, axis):
    return [x] + [swap(x, axis, distance) for distance in range(1, lax.axis_size(axis))]


def slots(x, axis):
    blocks = {0: x}
    for distance in reversed(distances(axis)):
        blocks.update({place ^ distance: swap(block, axis, distance) for place, block in list(blocks.items())})
    return [blocks[place] for place in range(len(blocks))]


def column(row):
    return jnp.transpose(jnp.broadcast_to(row, (LANES, LANES)))


def norm_kernel(features, *refs):
    me, squares, gain, *hidden, normed = refs
    rows, width = hidden[0].shape
    per_slot = width // LANES
    for top in range(0, rows, LANES):
        mean_square = squares[:, top : top + LANES] / features
        rooted = column(lax.rsqrt(mean_square + 1e-06))
        for slot in range(len(hidden)):
            owner = me[0] ^ slot
            for piece in range(per_slot):
                place = owner * per_slot + piece
                values = hidden[slot][top : top + LANES, piece * LANES : (piece + 1) * LANES]
                values = values.astype(jnp.float32) * rooted * gain[pl.ds(place, 1), :]
                normed[place, top : top + LANES, :] = values.astype(jnp.bfloat16)


def project_kernel(count, tokens, spots, *refs):
    me, ids, live = refs[:3]
    totals = refs[3 : 3 + count]
    normed = refs[3 + count]
    weights = refs[4 + count : 4 + count + spots]
    exact, delta, sums, means = refs[4 + count + spots : 8 + count + spots]
    scales, table, stretched, waves = refs[8 + count + spots :]
    step = pl.program_id(0)
    last = pl.num_programs(0) - 1
    rows = normed.shape[1]
    blocks = normed.shape[0]
    per_slot = blocks // count
    groups = HALF // GROUP

    def prepare(group, buffer):
        table[buffer] = jnp.transpose(scales[group])
        for ratio in range(RATIOS):
            stretched[buffer, ratio] = jnp.broadcast_to(table[buffer, :, ratio : ratio + 1], (LANES, LANES))

    def quantize(half, group, buffer):
        top = half * HALF + group * GROUP
        for spot in range(spots):
            wide = weights[spot][top : top + GROUP, :].astype(jnp.float32)
            for ratio in range(RATIOS):
                scaled = wide * stretched[buffer, ratio]
                peak = jnp.max(jnp.abs(scaled), axis=0, keepdims=True)
                unit = (peak + 1e-06) / 7.0
                level = scaled * (1.0 / unit)
                part = (level - jnp.round(level)).astype(jnp.bfloat16)
                square = part * part
                series = (square + jnp.bfloat16(LINEAR)) * square + jnp.bfloat16(CONSTANT)
                wave = series * (jnp.bfloat16(0.25) - square) * part
                wave = wave * (unit * GAIN).astype(jnp.bfloat16)
                waves[half, ratio, spot, group * GROUP : (group + 1) * GROUP, :] = wave

    def multiply(half, first):
        for ratio in range(RATIOS):
            left = []
            for group in range(groups):
                shrink = scales[first + group, RATIOS + ratio : RATIOS + ratio + 1, :]
                left.append(normed[first + group] * shrink.astype(jnp.bfloat16))
            right = jnp.concatenate([waves[half, ratio, spot] for spot in range(spots)], axis=1)
            delta[ratio] += jnp.dot(jnp.concatenate(left, axis=1), right, preferred_element_type=jnp.float32)

    @pl.when(step == 0)
    def _():
        for slot in range(count):
            owner = me[0] ^ slot
            for piece in range(per_slot):
                means[pl.ds(owner * per_slot + piece, 1), :] = totals[slot][piece : piece + 1, :]
        sums_all = means[...]
        logged = jnp.log(sums_all + 1e-06)
        centred = logged - 0.5 * (jnp.max(logged) + jnp.min(logged))
        means[...] = sums_all / tokens
        for ratio in range(RATIOS):
            alpha = ids[ratio].astype(jnp.float32) / GRID
            scale = jnp.exp(alpha * centred)
            scales[:, ratio, :] = scale
            scales[:, RATIOS + ratio, :] = 1.0 / scale
        exact[...] = jnp.zeros_like(exact)
        delta[...] = jnp.zeros_like(delta)
        waves[1] = jnp.zeros_like(waves[1])
        prepare(0, 0)

    base = step * 2 * groups
    for half in range(2):
        for group in range(groups):
            index = half * groups + group
            prepare(jnp.minimum(base + index + 1, blocks - 1), (index + 1) % 2)
            quantize(half, group, index % 2)
        multiply(1 - half, base if half else jnp.maximum(base - groups, 0))
    for half in range(2):
        left = jnp.concatenate([normed[base + half * groups + group] for group in range(groups)], axis=1)
        right = jnp.concatenate([weight[half * HALF : (half + 1) * HALF, :] for weight in weights], axis=1)
        exact[...] += jnp.dot(left, right, preferred_element_type=jnp.float32)

    @pl.when(step == last)
    def _():
        multiply(1, base + groups)
        masks = [column(live[:, top : top + LANES].astype(jnp.float32)) for top in range(0, rows, LANES)]
        for ratio in range(RATIOS + 1):
            gathered = jnp.zeros((1, LANES), jnp.float32)
            for index, top in enumerate(range(0, rows, LANES)):
                for at in range(0, exact.shape[1], LANES):
                    if ratio < RATIOS:
                        value = delta[ratio, top : top + LANES, at : at + LANES]
                    else:
                        value = exact[top : top + LANES, at : at + LANES]
                    value = value * masks[index]
                    gathered = gathered + jnp.sum(value * value, axis=0, keepdims=True)
            sums[ratio : ratio + 1, :] = gathered
        sums[RATIOS + 1 :, :] = jnp.zeros((8 - RATIOS - 1, LANES), jnp.float32)


def blend_kernel(first, second, exact, delta, losses, query, kv):
    sums = first[...] + second[...]
    folded = [jnp.sum(sums[ratio : ratio + 1, :], axis=1, keepdims=True) for ratio in range(RATIOS + 1)]
    loss = [folded[ratio] / folded[RATIOS] for ratio in range(RATIOS)]
    inverse = [1.0 / (value * value) for value in loss]
    whole = inverse[0]
    for ratio in range(1, RATIOS):
        whole = whole + inverse[ratio]
    blended = exact[...]
    for ratio in range(RATIOS):
        losses[ratio] = loss[ratio][0, 0]
        blended = blended - (inverse[ratio] / whole) * delta[ratio]
    blended = blended.astype(jnp.bfloat16)
    query[...] = blended[:, : query.shape[1]]
    kv[...] = blended[:, query.shape[1] :]


def project(me, ratio_ids, live, total_slots, normed, q_weight, kv_weight, tokens):
    blocks, rows, _ = normed.shape
    features = blocks * LANES
    columns = q_weight.shape[1] + kv_weight.shape[1]
    spots = columns // LANES
    block = 2 * HALF
    whole = lambda shape: pl.BlockSpec(shape, lambda i: (0,) * len(shape))
    scalar = pl.BlockSpec(memory_space=pltpu.SMEM)
    lane_tile = lambda tile: pl.BlockSpec((block, LANES), lambda i: (i, tile))
    weights, tiles = [], []
    for array in (q_weight, kv_weight):
        for tile in range(array.shape[1] // LANES):
            weights.append(array)
            tiles.append(lane_tile(tile))
    return pl.pallas_call(
        functools.partial(project_kernel, len(total_slots), tokens, spots),
        grid=(features // block,),
        in_specs=[scalar, scalar, whole((1, rows))]
        + [whole(part.shape) for part in total_slots]
        + [whole(normed.shape)]
        + tiles,
        out_specs=[
            whole((rows, columns)),
            whole((RATIOS, rows, columns)),
            whole((8, LANES)),
            whole((blocks, LANES)),
        ],
        out_shape=[
            jax.ShapeDtypeStruct((rows, columns), jnp.float32),
            jax.ShapeDtypeStruct((RATIOS, rows, columns), jnp.float32),
            jax.ShapeDtypeStruct((8, LANES), jnp.float32),
            jax.ShapeDtypeStruct((blocks, LANES), jnp.float32),
        ],
        scratch_shapes=[
            pltpu.VMEM((blocks, 8, LANES), jnp.float32),
            pltpu.VMEM((2, LANES, 8), jnp.float32),
            pltpu.VMEM((2, RATIOS, LANES, LANES), jnp.float32),
            pltpu.VMEM((2, RATIOS, spots, HALF, LANES), jnp.bfloat16),
        ],
        cost_estimate=pl.CostEstimate(flops=10 * rows * features * columns, bytes_accessed=8 * features * columns, transcendentals=0),
        name="project",
    )(me, ratio_ids, live, *total_slots, normed, *weights)


def per_device(hidden, live, norm_gain, q_weight, kv_weight, ratio_ids):
    rows, width = hidden.shape
    shards = lax.axis_size("mp")
    features = width * shards
    tokens = rows * lax.axis_size("dp")
    query, kv = q_weight.shape[1], kv_weight.shape[1]
    index = lax.axis_index("mp")
    me = index.reshape(1).astype(jnp.int32)

    values = hidden.astype(jnp.float32)
    squares = sum(peers(jnp.sum(values * values, axis=1).reshape(1, rows), "mp"))
    squares, late = lax.optimization_barrier((squares, hidden))
    hidden_slots = slots(late, "mp")
    gain_slice = lax.dynamic_slice_in_dim(norm_gain, index * width, width)
    scaling = lax.rsqrt(squares.reshape(rows, 1) / features + 1e-06)
    own = (values * scaling * gain_slice[None, :]).astype(jnp.bfloat16)
    live_rows = live.astype(jnp.float32)[:, None]
    sums = jnp.sum(jnp.abs(own.astype(jnp.float32)) * live_rows, axis=0)
    sums = total(sums.reshape(width // LANES, LANES), "dp")
    total_slots = peers(sums, "mp")

    scalar = pl.BlockSpec(memory_space=pltpu.SMEM)
    vector = pl.BlockSpec(memory_space=pltpu.VMEM)
    normed = pl.pallas_call(
        functools.partial(norm_kernel, features),
        in_specs=[scalar] + [vector] * (2 + shards),
        out_specs=vector,
        out_shape=jax.ShapeDtypeStruct((features // LANES, rows, LANES), jnp.bfloat16),
        cost_estimate=pl.CostEstimate(flops=4 * rows * features, bytes_accessed=4 * rows * features, transcendentals=0),
        name="norm",
    )(me, squares, norm_gain.reshape(features // LANES, LANES), *hidden_slots)
    exact, delta, sums, means = project(
        me, ratio_ids, live.reshape(1, rows), total_slots, normed, q_weight, kv_weight, float(tokens)
    )
    sums = sum(peers(sums, "mp"))
    *steps, final = distances("dp")
    for distance in steps:
        sums = sums + swap(sums, "dp", distance)
    losses, q_latent, kv_latent = pl.pallas_call(
        blend_kernel,
        out_shape=[
            jax.ShapeDtypeStruct((RATIOS,), jnp.float32),
            jax.ShapeDtypeStruct((rows, query), jnp.bfloat16),
            jax.ShapeDtypeStruct((rows, kv), jnp.bfloat16),
        ],
        out_specs=[scalar, vector, vector],
        name="blend",
    )(sums, swap(sums, "dp", final), exact, delta)
    return losses, q_latent, kv_latent, means.reshape(features)


def solution(mesh):
    placed = (P("dp", "mp"), P("dp"), P(), P(None, "mp"), P(None, "mp"), P())
    return jax.shard_map(
        per_device,
        mesh=mesh,
        in_specs=placed,
        out_specs=(P(), P("dp", "mp"), P("dp", "mp"), P()),
        check_vma=False,
    )
```

time: 110 us -> 91.1 us (0.83)
  Pallas kernels: 54.8 us -> 41.5 us
  waiting for transfers between devices: 25.2 us -> 22.6 us
  starting transfers between devices: 21.4 us -> 19.1 us
    pallas_call x2 -> x3, Pallas kernels: 54.8 us -> 41.5 us  [the longest x1 36 us: project(): pl.pallas_call(functools.partial(project_kernel, len(total_slots), tokens...]
    ppermute x16 -> x18, waiting for transfers between devices: 25.2 us -> 22.6 us  [swap(): return lax.ppermute(x, axis, [(i, i ^ distance) for i in range(size)])]
    ppermute x16 -> x18, starting transfers between devices: 21.4 us -> 19.1 us  [swap(): return lax.ppermute(x, axis, [(i, i ^ distance) for i in range(size)])]
    slice x1 -> x0, local copies, waits for them, and re-layouts: 1.31 us -> none  [per_device(): return (losses[:, 0], q_latent, kv_latent, means.reshape(features))]
    add x9 -> x3, other arithmetic: 1.28 us -> 0.01 us  [total(): x = x + swap(x, axis, distance)]
    unnamed x14 -> x20, local copies, waits for them, and re-layouts: 0.89 us -> 2.11 us
  transfers between devices with their start and end apart: 16 -> 18, of which waited for: 11 -> 10; matrix products, arithmetic and copies ran while one was open for 3% -> 3% of each run, Pallas kernels for 0% -> 4%
where the time goes in v2:
time: 91.1 us; the launch traced here: 90.7 us
  Pallas kernels  41.5 us (46%)
  waiting for transfers between devices  22.6 us (25%)
  starting transfers between devices  19.1 us (21%)
  other arithmetic  3.85 us (4%)
  local copies, waits for them, and re-layouts  2.89 us (3%)
    pallas_call x1, Pallas kernels, project(): pl.pallas_call(functools.partial(project_kernel, len(total_slots), tokens...  36 us
    ppermute x18, waiting for transfers between devices, swap(): return lax.ppermute(x, axis, [(i, i ^ distance) for i in range(size)])  22.6 us
    ppermute x18, starting transfers between devices, swap(): return lax.ppermute(x, axis, [(i, i ^ distance) for i in range(size)])  19.1 us
    pallas_call x1, Pallas kernels, per_device(): pl.pallas_call(functools.partial(norm_kernel, features), in_specs=[scalar...  3.23 us
    pallas_call x1, Pallas kernels, per_device(): pl.pallas_call(blend_kernel, out_shape=[jax.ShapeDtypeStruct((RATIOS,), j...  2.21 us
    unnamed x20, local copies, waits for them, and re-layouts  2.11 us
  transfers between devices with their start and end apart: 18, of which 10 were waited for; matrix products, arithmetic and copies ran while one was open for 3% of the time, Pallas kernels for 4%

profile of v2, /device:TPU:0, one launch (start us, length us, event | category | flops | bytes accessed | tf_op | source)
XLA Modules:
  0.0 90.7 jit_solution(11210612324957606740)
XLA Ops:
  0.6 1.2 %fusion = f32[128]{0:T(128)S(1)} fusion(bf16[128,1792]{1,0:T(8,128)(2,1)} %refs_3_), kind=kLoop, calls=%fused_computation.2 | loop fusion | flops 688000 | bytes 459264 | tf_op jit(solution)/shard_map/reduce_sum | solution.py:231
  1.8 3.0 %collective-permute-start.1 = (f32[1,128]{1,0:T(1,128)S(1)}, f32[1,128]{1,0:T(1,128)S(1)}, u32[]{:S(2)}, u32[]{:S(2)}) collective-permute-start(f32[1,128]{1,0:T(1,128)S(1)} %bitcast.14), channel_id=1, source_target_pairs={{0,2},{1,3},{2,0},{3,1},{4,6},{5,7},{6,4},{7,5},{8,10},{9,11},{10,... | collective-permute-start | bytes 1544 | tf_op jit(solution)/shard_map/ppermute | solution.py:20
  4.8 0.0 collective-permute-start.2
  4.9 0.2 collective-permute-start
  5.0 1.4 %collective-permute-done.1 = f32[1,128]{1,0:T(1,128)S(1)} collective-permute-done((f32[1,128]{1,0:T(1,128)S(1)}, f32[1,128]{1,0:T(1,128)S(1)}, u32[]{:S(2)}, u32[]{:S(2)}) %collective-permute-start.1) | collective-permute-done | bytes 544 | tf_op jit(solution)/shard_map/ppermute | solution.py:20
  6.4 1.4 %collective-permute-done.2 = f32[1,128]{1,0:T(1,128)S(1)} collective-permute-done((f32[1,128]{1,0:T(1,128)S(1)}, f32[1,128]{1,0:T(1,128)S(1)}, u32[]{:S(2)}, u32[]{:S(2)}) %collective-permute-start.2) | collective-permute-done | bytes 544 | tf_op jit(solution)/shard_map/ppermute | solution.py:20
  7.8 0.0 collective-permute-done
  7.9 0.0 copy-start.9
  7.9 0.6 collective-permute-start.10
  8.5 0.7 convert_element_type.15
  9.2 0.8 dynamic_slice.3
  10.0 1.3 %multiply_reduce_fusion = f32[1792]{0:T(1024)S(1)} fusion(bf16[128,1792]{1,0:T(8,128)(2,1)} %refs_3_, f32[128]{0:T(128)S(1)} %convert_element_type.15, f32[1792]{0:T(1024)S(1)} %dynamic_slice.3, f32[128]{0:T(128)S(1)} %rsqrt_bitcast_fusion), kind=kLoop, calls=%fused_computation.5 | loop fusion | flops 1833216 | bytes 474112 | tf_op jit(solution)/shard_map/reduce_sum | solution.py:238
  11.2 1.6 %collective-permute-start.3 = (f32[14,128]{1,0:T(8,128)S(1)}, f32[14,128]{1,0:T(8,128)S(1)}, u32[]{:S(2)}, u32[]{:S(2)}) collective-permute-start(f32[14,128]{1,0:T(8,128)S(1)} %bitcast.12), channel_id=1, source_target_pairs={{0,4},{4,0},{8,12},{12,8},{16,20},{20,16},{24,28},{28,24},{1,5},{5... | collective-permute-start | bytes 21512 | tf_op jit(solution)/shard_map/ppermute | solution.py:20
  12.8 0.0 collective-permute-start.9
  12.8 7.3 %collective-permute-done.10.refs_5_ = bf16[128,1792]{1,0:T(8,128)(2,1)S(1)} collective-permute-done((bf16[128,1792]{1,0:T(8,128)(2,1)}, bf16[128,1792]{1,0:T(8,128)(2,1)S(1)}, u32[]{:S(2)}, u32[]{:S(2)}) %collective-permute-start.10) | collective-permute-done | bytes 458784 | tf_op jit(solution)/shard_map/ppermute | solution.py:20
  20.1 0.0 copy-start
  20.1 0.0 collective-permute-start.11
  20.1 0.0 collective-permute-done.3
  20.1 1.6 %collective-permute-start.4 = (f32[14,128]{1,0:T(8,128)S(1)}, f32[14,128]{1,0:T(8,128)S(1)}, u32[]{:S(2)}, u32[]{:S(2)}) collective-permute-start(f32[14,128]{1,0:T(8,128)S(1)} %bitcast_add_fusion), channel_id=1, source_target_pairs={{0,8},{4,12},{8,0},{12,4},{16,24},{20,28},{24,16},{28,20},{1,9},{5... | collective-permute-start | bytes 21512 | tf_op jit(solution)/shard_map/ppermute | solution.py:20
  21.8 2.1 %collective-permute-done.4 = f32[14,128]{1,0:T(8,128)S(1)} collective-permute-done((f32[14,128]{1,0:T(8,128)S(1)}, f32[14,128]{1,0:T(8,128)S(1)}, u32[]{:S(2)}, u32[]{:S(2)}) %collective-permute-start.4) | collective-permute-done | bytes 7200 | tf_op jit(solution)/shard_map/ppermute | solution.py:20
  23.9 2.6 %collective-permute-start.5 = (f32[14,128]{1,0:T(8,128)S(1)}, f32[14,128]{1,0:T(8,128)S(1)}, u32[]{:S(2)}, u32[]{:S(2)}) collective-permute-start(f32[14,128]{1,0:T(8,128)S(1)} %fusion.3), channel_id=1, source_target_pairs={{0,16},{4,20},{8,24},{12,28},{16,0},{20,4},{24,8},{28,12},{1,17},{... | collective-permute-start | bytes 21512 | tf_op jit(solution)/shard_map/ppermute | solution.py:20
  26.5 2.0 %collective-permute-done.5 = f32[14,128]{1,0:T(8,128)S(1)} collective-permute-done((f32[14,128]{1,0:T(8,128)S(1)}, f32[14,128]{1,0:T(8,128)S(1)}, u32[]{:S(2)}, u32[]{:S(2)}) %collective-permute-start.5) | collective-permute-done | bytes 7200 | tf_op jit(solution)/shard_map/ppermute | solution.py:20
  28.4 0.0 copy-start.3
  28.4 0.0 collective-permute-start.8
  28.4 0.9 %collective-permute-start.7 = (f32[14,128]{1,0:T(8,128)S(1)}, f32[14,128]{1,0:T(8,128)S(1)}, u32[]{:S(2)}, u32[]{:S(2)}) collective-permute-start(f32[14,128]{1,0:T(8,128)S(1)} %add.56.refs_3_), channel_id=1, source_target_pairs={{0,2},{1,3},{2,0},{3,1},{4,6},{5,7},{6,4},{7,5},{8,10},{9,11},{10,... | collective-permute-start | bytes 21512 | tf_op jit(solution)/shard_map/ppermute | solution.py:20
  29.3 0.9 %collective-permute-start.6 = (f32[14,128]{1,0:T(8,128)S(1)}, f32[14,128]{1,0:T(8,128)S(1)}, u32[]{:S(2)}, u32[]{:S(2)}) collective-permute-start(f32[14,128]{1,0:T(8,128)S(1)} %add.56.refs_3_), channel_id=1, source_target_pairs={{0,1},{1,0},{2,3},{3,2},{4,5},{5,4},{6,7},{7,6},{8,9},{9,8},{10,11... | collective-permute-start | bytes 21512 | tf_op jit(solution)/shard_map/ppermute | solution.py:20
  30.3 0.0 collective-permute-done.9.refs_4_
  30.3 0.0 copy-start.1
  30.3 0.0 collective-permute-done.11.refs_6_
  30.3 0.0 copy-start.2
  30.3 0.0 copy-done.9
  30.3 0.0 copy-done
  30.3 0.7 copy-done.1
  31.1 0.2 copy-done.2
  31.2 3.2 %norm.1.refs_7_ = bf16[56,128,128]{2,1,0:T(8,128)(2,1)} custom-call(s32[1]{0:T(128)} %bitcast.refs_0_, f32[1,128]{1,0:T(1,128)} %copy-done.9, f32[56,128]{1,0:T(8,128)} %bitcast.13, bf16[128,1792]{1,0:T(8,128)(2,1)} %refs_3_, bf16[128,1792]{1,0:T(8,128)(2,1)} %copy-done.1, bf16[128,1792]{1,0:T(8,128)(2,1)} %copy-done, bf16[128,1792]{1,0:T(8,128)(2,1)} %copy-done.2), custom_call_target="tpu_custom_call" | custom-call | flops 3670016 | bytes 3670016 | tf_op jit(solution)/shard_map/norm/pallas_call | solution.py:244
  34.5 0.0 collective-permute-done.8.refs_6_
  34.5 0.0 copy-start.5
  34.5 0.0 collective-permute-done.7.refs_5_
  34.5 0.0 copy-start.6
  34.5 0.0 collective-permute-done.6.refs_4_
  34.5 0.0 copy-start.7
  34.5 0.0 copy-done.3
  34.5 0.5 copy-done.5
  35.1 0.0 copy-done.6
  35.1 0.0 copy-done.7
  35.1 36.0 %project.1 = (f32[128,512]{1,0:T(8,128)}, f32[4,128,512]{2,1,0:T(8,128)}, f32[8,128]{1,0:T(8,128)}, f32[56,128]{1,0:T(8,128)}) custom-call(s32[1]{0:T(128)} %bitcast.refs_0_, s32[4]{0:T(128)} %refs_1_.1, s32[1,128]{1,0:T(1,128)} %bitcast.17, f32[14,128]{1,0:T(8,128)} %copy-done.3, f32[14,128]{1,0:T(8,128)} %copy-done.7, f32[14,128]{1,0:T(8,128)} %copy-done.6, ...), custom_call_target="tpu_custom_call" | custom-call | flops 4697620480 | bytes 29360128 | tf_op jit(solution)/shard_map/project/pallas_call | solution.py:191
  71.1 0.5 collective-permute-start.14
  71.7 1.2 %collective-permute-start.13 = (f32[8,128]{1,0:T(8,128)}, f32[8,128]{1,0:T(8,128)S(1)}, u32[]{:S(2)}, u32[]{:S(2)}) collective-permute-start(f32[8,128]{1,0:T(8,128)} %get-tuple-element.15), channel_id=1, source_target_pairs={{0,2},{1,3},{2,0},{3,1},{4,6},{5,7},{6,4},{7,5},{8,10},{9,11},{10,... | collective-permute-start | bytes 12296 | tf_op jit(solution)/shard_map/ppermute | solution.py:20
  72.8 0.2 collective-permute-start.12
  73.1 1.4 %collective-permute-done.14 = f32[8,128]{1,0:T(8,128)S(1)} collective-permute-done((f32[8,128]{1,0:T(8,128)}, f32[8,128]{1,0:T(8,128)S(1)}, u32[]{:S(2)}, u32[]{:S(2)}) %collective-permute-start.14) | collective-permute-done | bytes 4128 | tf_op jit(solution)/shard_map/ppermute | solution.py:20
  74.5 1.0 %collective-permute-done.13 = f32[8,128]{1,0:T(8,128)S(1)} collective-permute-done((f32[8,128]{1,0:T(8,128)}, f32[8,128]{1,0:T(8,128)S(1)}, u32[]{:S(2)}, u32[]{:S(2)}) %collective-permute-start.13) | collective-permute-done | bytes 4128 | tf_op jit(solution)/shard_map/ppermute | solution.py:20
  75.5 0.0 collective-permute-done.12
  75.5 0.7 add_add_fusion
  76.2 1.5 %collective-permute-start.15 = (f32[8,128]{1,0:T(8,128)S(1)}, f32[8,128]{1,0:T(8,128)S(1)}, u32[]{:S(2)}, u32[]{:S(2)}) collective-permute-start(f32[8,128]{1,0:T(8,128)S(1)} %add_add_fusion), channel_id=1, source_target_pairs={{0,4},{4,0},{8,12},{12,8},{16,20},{20,16},{24,28},{28,24},{1,5},{5... | collective-permute-start | bytes 12296 | tf_op jit(solution)/shard_map/ppermute | solution.py:20
  77.7 2.1 %collective-permute-done.15 = f32[8,128]{1,0:T(8,128)S(1)} collective-permute-done((f32[8,128]{1,0:T(8,128)S(1)}, f32[8,128]{1,0:T(8,128)S(1)}, u32[]{:S(2)}, u32[]{:S(2)}) %collective-permute-start.15) | collective-permute-done | bytes 4128 | tf_op jit(solution)/shard_map/ppermute | solution.py:20
  79.8 1.6 %collective-permute-start.16 = (f32[8,128]{1,0:T(8,128)S(1)}, f32[8,128]{1,0:T(8,128)S(1)}, u32[]{:S(2)}, u32[]{:S(2)}) collective-permute-start(f32[8,128]{1,0:T(8,128)S(1)} %add.60), channel_id=1, source_target_pairs={{0,8},{4,12},{8,0},{12,4},{16,24},{20,28},{24,16},{28,20},{1,9},{5... | collective-permute-start | bytes 12296 | tf_op jit(solution)/shard_map/ppermute | solution.py:20
  81.4 2.0 %collective-permute-done.16 = f32[8,128]{1,0:T(8,128)S(1)} collective-permute-done((f32[8,128]{1,0:T(8,128)S(1)}, f32[8,128]{1,0:T(8,128)S(1)}, u32[]{:S(2)}, u32[]{:S(2)}) %collective-permute-start.16) | collective-permute-done | bytes 4128 | tf_op jit(solution)/shard_map/ppermute | solution.py:20
  83.4 0.0 copy-start.4
  83.4 2.6 %collective-permute-start.17 = (f32[8,128]{1,0:T(8,128)S(1)}, f32[8,128]{1,0:T(8,128)S(1)}, u32[]{:S(2)}, u32[]{:S(2)}) collective-permute-start(f32[8,128]{1,0:T(8,128)S(1)} %add.61.first), channel_id=1, source_target_pairs={{0,16},{4,20},{8,24},{12,28},{16,0},{20,4},{24,8},{28,12},{1,17},{... | collective-permute-start | bytes 12296 | tf_op jit(solution)/shard_map/ppermute | solution.py:20
  86.0 1.9 %collective-permute-done.17.second = f32[8,128]{1,0:T(8,128)S(1)} collective-permute-done((f32[8,128]{1,0:T(8,128)S(1)}, f32[8,128]{1,0:T(8,128)S(1)}, u32[]{:S(2)}, u32[]{:S(2)}) %collective-permute-start.17) | collective-permute-done | bytes 4128 | tf_op jit(solution)/shard_map/ppermute | solution.py:20
  87.9 0.0 copy-start.8
  87.9 0.0 copy-done.4
  87.9 0.6 copy-done.8
  88.5 2.2 %blend.1 = (f32[4]{0:T(128)}, bf16[128,384]{1,0:T(8,128)(2,1)}, bf16[128,128]{1,0:T(8,128)(2,1)}) custom-call(f32[8,128]{1,0:T(8,128)} %copy-done.4, f32[8,128]{1,0:T(8,128)} %copy-done.8, f32[128,512]{1,0:T(8,128)} %get-tuple-element.16.exact, f32[4,128,512]{2,1,0:T(8,128)} %get-tuple-element.17.delta), custom_call_target="tpu_custom_call" | custom-call | tf_op jit(solution)/shard_map/blend/pallas_call | solution.py:259
  (7 shorter events, 0.0 us)
Async XLA Ops:
  1.8 4.6 %collective-permute-start.1 = (f32[1,128]{1,0:T(1,128)S(1)}, f32[1,128]{1,0:T(1,128)S(1)}, u32[]{:S(2)}, u32[]{:S(2)}) collective-permute-start(f32[1,128]{1,0:T(1,128)S(1)} %bitcast.14), channel_id=1, source_target_pairs={{0,2},{1,3},{2,0},{3,1},{4,6},{5,7},{6,4},{7,5},{8,10},{9,11},{10,... | collective-permute-start | bytes 1544 | tf_op jit(solution)/shard_map/ppermute | solution.py:20
  4.8 3.0 %collective-permute-start.2 = (f32[1,128]{1,0:T(1,128)S(1)}, f32[1,128]{1,0:T(1,128)S(1)}, u32[]{:S(2)}, u32[]{:S(2)}) collective-permute-start(f32[1,128]{1,0:T(1,128)S(1)} %bitcast.15), channel_id=1, source_target_pairs={{0,3},{1,2},{2,1},{3,0},{4,7},{5,6},{6,5},{7,4},{8,11},{9,10},{10,... | collective-permute-start | bytes 1544 | tf_op jit(solution)/shard_map/ppermute | solution.py:20
  4.9 3.0 %collective-permute-start = (f32[1,128]{1,0:T(1,128)S(1)}, f32[1,128]{1,0:T(1,128)S(1)}, u32[]{:S(2)}, u32[]{:S(2)}) collective-permute-start(f32[1,128]{1,0:T(1,128)S(1)} %bitcast.16), channel_id=1, source_target_pairs={{0,1},{1,0},{2,3},{3,2},{4,5},{5,4},{6,7},{7,6},{8,9},{9,8},{10,11... | collective-permute-start | bytes 1544 | tf_op jit(solution)/shard_map/ppermute | solution.py:20
  7.9 22.5 %copy-start.9 = (f32[1,128]{1,0:T(1,128)}, f32[1,128]{1,0:T(1,128)S(1)}, u32[]{:S(2)}) copy-start(f32[1,128]{1,0:T(1,128)S(1)} %add_add_fusion.1.refs_1_) | copy-start | bytes 1540
  7.9 12.3 %collective-permute-start.10 = (bf16[128,1792]{1,0:T(8,128)(2,1)}, bf16[128,1792]{1,0:T(8,128)(2,1)S(1)}, u32[]{:S(2)}, u32[]{:S(2)}) collective-permute-start(bf16[128,1792]{1,0:T(8,128)(2,1)} %refs_3_), channel_id=1, source_target_pairs={{0,2},{1,3},{2,0},{3,1},{4,6},{5,7},{6,4},{7,5},{8,10},{9,11},{10,... | collective-permute-start | bytes 1376264 | tf_op jit(solution)/shard_map/ppermute | solution.py:20
  11.2 8.9 %collective-permute-start.3 = (f32[14,128]{1,0:T(8,128)S(1)}, f32[14,128]{1,0:T(8,128)S(1)}, u32[]{:S(2)}, u32[]{:S(2)}) collective-permute-start(f32[14,128]{1,0:T(8,128)S(1)} %bitcast.12), channel_id=1, source_target_pairs={{0,4},{4,0},{8,12},{12,8},{16,20},{20,16},{24,28},{28,24},{1,5},{5... | collective-permute-start | bytes 21512 | tf_op jit(solution)/shard_map/ppermute | solution.py:20
  12.8 17.5 %collective-permute-start.9 = (bf16[128,1792]{1,0:T(8,128)(2,1)}, bf16[128,1792]{1,0:T(8,128)(2,1)S(1)}, u32[]{:S(2)}, u32[]{:S(2)}) collective-permute-start(bf16[128,1792]{1,0:T(8,128)(2,1)} %refs_3_), channel_id=1, source_target_pairs={{0,1},{1,0},{2,3},{3,2},{4,5},{5,4},{6,7},{7,6},{8,9},{9,8},{10,11... | collective-permute-start | bytes 1376264 | tf_op jit(solution)/shard_map/ppermute | solution.py:20
  20.1 10.2 %copy-start = (bf16[128,1792]{1,0:T(8,128)(2,1)}, bf16[128,1792]{1,0:T(8,128)(2,1)S(1)}, u32[]{:S(2)}) copy-start(bf16[128,1792]{1,0:T(8,128)(2,1)S(1)} %collective-permute-done.10.refs_5_) | copy-start | bytes 1376260
  20.1 10.2 %collective-permute-start.11 = (bf16[128,1792]{1,0:T(8,128)(2,1)S(1)}, bf16[128,1792]{1,0:T(8,128)(2,1)S(1)}, u32[]{:S(2)}, u32[]{:S(2)}) collective-permute-start(bf16[128,1792]{1,0:T(8,128)(2,1)S(1)} %collective-permute-done.10.refs_5_), channel_id=1, source_target_pairs={{0,1},{1,0},{2,3},{3,2},{4,5},{5,4},{6,7},{7,6},{8,9},{9,8},{10,11... | collective-permute-start | bytes 1376264 | tf_op jit(solution)/shard_map/ppermute | solution.py:20
  20.1 3.7 %collective-permute-start.4 = (f32[14,128]{1,0:T(8,128)S(1)}, f32[14,128]{1,0:T(8,128)S(1)}, u32[]{:S(2)}, u32[]{:S(2)}) collective-permute-start(f32[14,128]{1,0:T(8,128)S(1)} %bitcast_add_fusion), channel_id=1, source_target_pairs={{0,8},{4,12},{8,0},{12,4},{16,24},{20,28},{24,16},{28,20},{1,9},{5... | collective-permute-start | bytes 21512 | tf_op jit(solution)/shard_map/ppermute | solution.py:20
  23.9 4.5 %collective-permute-start.5 = (f32[14,128]{1,0:T(8,128)S(1)}, f32[14,128]{1,0:T(8,128)S(1)}, u32[]{:S(2)}, u32[]{:S(2)}) collective-permute-start(f32[14,128]{1,0:T(8,128)S(1)} %fusion.3), channel_id=1, source_target_pairs={{0,16},{4,20},{8,24},{12,28},{16,0},{20,4},{24,8},{28,12},{1,17},{... | collective-permute-start | bytes 21512 | tf_op jit(solution)/shard_map/ppermute | solution.py:20
  28.4 6.1 %copy-start.3 = (f32[14,128]{1,0:T(8,128)}, f32[14,128]{1,0:T(8,128)S(1)}, u32[]{:S(2)}) copy-start(f32[14,128]{1,0:T(8,128)S(1)} %add.56.refs_3_) | copy-start | bytes 21508
  28.4 6.1 %collective-permute-start.8 = (f32[14,128]{1,0:T(8,128)S(1)}, f32[14,128]{1,0:T(8,128)S(1)}, u32[]{:S(2)}, u32[]{:S(2)}) collective-permute-start(f32[14,128]{1,0:T(8,128)S(1)} %add.56.refs_3_), channel_id=1, source_target_pairs={{0,3},{1,2},{2,1},{3,0},{4,7},{5,6},{6,5},{7,4},{8,11},{9,10},{10,... | collective-permute-start | bytes 21512 | tf_op jit(solution)/shard_map/ppermute | solution.py:20
  28.4 6.1 %collective-permute-start.7 = (f32[14,128]{1,0:T(8,128)S(1)}, f32[14,128]{1,0:T(8,128)S(1)}, u32[]{:S(2)}, u32[]{:S(2)}) collective-permute-start(f32[14,128]{1,0:T(8,128)S(1)} %add.56.refs_3_), channel_id=1, source_target_pairs={{0,2},{1,3},{2,0},{3,1},{4,6},{5,7},{6,4},{7,5},{8,10},{9,11},{10,... | collective-permute-start | bytes 21512 | tf_op jit(solution)/shard_map/ppermute | solution.py:20
  29.3 5.2 %collective-permute-start.6 = (f32[14,128]{1,0:T(8,128)S(1)}, f32[14,128]{1,0:T(8,128)S(1)}, u32[]{:S(2)}, u32[]{:S(2)}) collective-permute-start(f32[14,128]{1,0:T(8,128)S(1)} %add.56.refs_3_), channel_id=1, source_target_pairs={{0,1},{1,0},{2,3},{3,2},{4,5},{5,4},{6,7},{7,6},{8,9},{9,8},{10,11... | collective-permute-start | bytes 21512 | tf_op jit(solution)/shard_map/ppermute | solution.py:20
  30.3 0.8 copy-start.1
  30.3 0.9 %copy-start.2 = (bf16[128,1792]{1,0:T(8,128)(2,1)}, bf16[128,1792]{1,0:T(8,128)(2,1)S(1)}, u32[]{:S(2)}) copy-start(bf16[128,1792]{1,0:T(8,128)(2,1)S(1)} %collective-permute-done.11.refs_6_) | copy-start | bytes 1376260
  34.5 0.6 copy-start.5
  34.5 0.6 copy-start.6
  34.5 0.6 copy-start.7
  71.1 3.3 %collective-permute-start.14 = (f32[8,128]{1,0:T(8,128)}, f32[8,128]{1,0:T(8,128)S(1)}, u32[]{:S(2)}, u32[]{:S(2)}) collective-permute-start(f32[8,128]{1,0:T(8,128)} %get-tuple-element.15), channel_id=1, source_target_pairs={{0,3},{1,2},{2,1},{3,0},{4,7},{5,6},{6,5},{7,4},{8,11},{9,10},{10,... | collective-permute-start | bytes 12296 | tf_op jit(solution)/shard_map/ppermute | solution.py:20
  71.7 3.8 %collective-permute-start.13 = (f32[8,128]{1,0:T(8,128)}, f32[8,128]{1,0:T(8,128)S(1)}, u32[]{:S(2)}, u32[]{:S(2)}) collective-permute-start(f32[8,128]{1,0:T(8,128)} %get-tuple-element.15), channel_id=1, source_target_pairs={{0,2},{1,3},{2,0},{3,1},{4,6},{5,7},{6,4},{7,5},{8,10},{9,11},{10,... | collective-permute-start | bytes 12296 | tf_op jit(solution)/shard_map/ppermute | solution.py:20
  72.8 2.6 %collective-permute-start.12 = (f32[8,128]{1,0:T(8,128)}, f32[8,128]{1,0:T(8,128)S(1)}, u32[]{:S(2)}, u32[]{:S(2)}) collective-permute-start(f32[8,128]{1,0:T(8,128)} %get-tuple-element.15), channel_id=1, source_target_pairs={{0,1},{1,0},{2,3},{3,2},{4,5},{5,4},{6,7},{7,6},{8,9},{9,8},{10,11... | collective-permute-start | bytes 12296 | tf_op jit(solution)/shard_map/ppermute | solution.py:20
  76.2 3.6 %collective-permute-start.15 = (f32[8,128]{1,0:T(8,128)S(1)}, f32[8,128]{1,0:T(8,128)S(1)}, u32[]{:S(2)}, u32[]{:S(2)}) collective-permute-start(f32[8,128]{1,0:T(8,128)S(1)} %add_add_fusion), channel_id=1, source_target_pairs={{0,4},{4,0},{8,12},{12,8},{16,20},{20,16},{24,28},{28,24},{1,5},{5... | collective-permute-start | bytes 12296 | tf_op jit(solution)/shard_map/ppermute | solution.py:20
  79.8 3.6 %collective-permute-start.16 = (f32[8,128]{1,0:T(8,128)S(1)}, f32[8,128]{1,0:T(8,128)S(1)}, u32[]{:S(2)}, u32[]{:S(2)}) collective-permute-start(f32[8,128]{1,0:T(8,128)S(1)} %add.60), channel_id=1, source_target_pairs={{0,8},{4,12},{8,0},{12,4},{16,24},{20,28},{24,16},{28,20},{1,9},{5... | collective-permute-start | bytes 12296 | tf_op jit(solution)/shard_map/ppermute | solution.py:20
  83.4 4.5 %copy-start.4 = (f32[8,128]{1,0:T(8,128)}, f32[8,128]{1,0:T(8,128)S(1)}, u32[]{:S(2)}) copy-start(f32[8,128]{1,0:T(8,128)S(1)} %add.61.first) | copy-start | bytes 12292
  83.4 4.5 %collective-permute-start.17 = (f32[8,128]{1,0:T(8,128)S(1)}, f32[8,128]{1,0:T(8,128)S(1)}, u32[]{:S(2)}, u32[]{:S(2)}) collective-permute-start(f32[8,128]{1,0:T(8,128)S(1)} %add.61.first), channel_id=1, source_target_pairs={{0,16},{4,20},{8,24},{12,28},{16,0},{20,4},{24,8},{28,12},{1,17},{... | collective-permute-start | bytes 12296 | tf_op jit(solution)/shard_map/ppermute | solution.py:20
  87.9 0.6 copy-start.8

commit v3 on v2

v3 whole, which is shorter than its diff:
```python
import functools

import jax
import jax.numpy as jnp
from jax import lax
from jax.experimental import pallas as pl
from jax.experimental.pallas import tpu as pltpu
from jax.sharding import PartitionSpec as P

GROUP = 128
GRID = 20
RATIOS = 4
LANES = 128
HALF = 256
LINEAR, CONSTANT, GAIN = -1.1640625, 0.458984375, 8.705


def swap(x, axis, distance):
    size = lax.axis_size(axis)
    return lax.ppermute(x, axis, [(i, i ^ distance) for i in range(size)])


def distances(axis):
    size = lax.axis_size(axis)
    assert size & (size - 1) == 0
    return [1 << bit for bit in range(size.bit_length() - 1)]


def total(x, axis):
    for distance in distances(axis):
        x = x + swap(x, axis, distance)
    return x


def peers(x, axis):
    return [x] + [swap(x, axis, distance) for distance in range(1, lax.axis_size(axis))]


def column(row):
    return jnp.transpose(jnp.broadcast_to(row, (LANES, LANES)))


def squares_kernel(hidden, live, gain, squares, kept, mask, kept_gain):
    kept[...] = hidden[...]
    kept_gain[...] = gain[...]
    mask[...] = live[...].astype(jnp.float32)
    for top in range(0, hidden.shape[0], LANES):
        gathered = jnp.zeros((LANES, LANES), jnp.float32)
        for at in range(0, hidden.shape[1], LANES):
            values = hidden[top : top + LANES, at : at + LANES].astype(jnp.float32)
            gathered = gathered + values * values
        squares[:, top : top + LANES] = jnp.sum(jnp.transpose(gathered), axis=0, keepdims=True)


def stats_kernel(features, me, squares, live, gain, hidden, sums):
    rows, width = hidden.shape
    per_slot = width // LANES
    for piece in range(per_slot):
        row = gain[pl.ds(me[0] * per_slot + piece, 1), :]
        gathered = jnp.zeros((1, LANES), jnp.float32)
        for top in range(0, rows, LANES):
            rooted = column(lax.rsqrt(squares[:, top : top + LANES] / features + 1e-06))
            mask = column(live[:, top : top + LANES])
            values = hidden[top : top + LANES, piece * LANES : (piece + 1) * LANES].astype(jnp.float32)
            values = (values * rooted * row).astype(jnp.bfloat16).astype(jnp.float32)
            gathered = gathered + jnp.sum(jnp.abs(values) * mask, axis=0, keepdims=True)
        sums[piece : piece + 1, :] = gathered


def norm_kernel(features, *refs):
    me, squares, gain, *hidden, normed = refs
    rows, width = hidden[0].shape
    per_slot = width // LANES
    for top in range(0, rows, LANES):
        mean_square = squares[:, top : top + LANES] / features
        rooted = column(lax.rsqrt(mean_square + 1e-06))
        for slot in range(len(hidden)):
            owner = me[0] ^ slot
            for piece in range(per_slot):
                place = owner * per_slot + piece
                values = hidden[slot][top : top + LANES, piece * LANES : (piece + 1) * LANES]
                values = values.astype(jnp.float32) * rooted * gain[pl.ds(place, 1), :]
                normed[place, top : top + LANES, :] = values.astype(jnp.bfloat16)


def project_kernel(count, tokens, *refs):
    me, ids, live = refs[:3]
    totals = refs[3 : 3 + count]
    normed, query, kv = refs[3 + count : 6 + count]
    exact, delta, sums, means = refs[6 + count : 10 + count]
    scales, table, stretched, waves, held, arrivals = refs[10 + count :]
    rows = normed.shape[1]
    blocks = normed.shape[0]
    per_slot = blocks // count
    groups = HALF // GROUP
    parts = [(ref, at) for ref in (query, kv) for at in range(0, ref.shape[1], LANES)]
    steps = blocks // (2 * groups)

    def fetches(step):
        slot = lax.rem(step, 2)
        span = pl.ds(pl.multiple_of(step * 2 * HALF, 2 * HALF), 2 * HALF)
        return [
            pltpu.make_async_copy(ref.at[span, pl.ds(at, LANES)], held.at[slot, spot], arrivals.at[slot, spot])
            for spot, (ref, at) in enumerate(parts)
        ]

    def prepare(group, buffer):
        table[buffer] = jnp.transpose(scales[group])
        for ratio in range(RATIOS):
            stretched[buffer, ratio] = jnp.broadcast_to(table[buffer, :, ratio : ratio + 1], (LANES, LANES))

    def quantize(half, group, buffer, slot):
        top = half * HALF + group * GROUP
        for spot in range(len(parts)):
            wide = held[slot, spot, top : top + GROUP, :].astype(jnp.float32)
            for ratio in range(RATIOS):
                scaled = wide * stretched[buffer, ratio]
                peak = jnp.max(jnp.abs(scaled), axis=0, keepdims=True) + 1e-06
                level = scaled * (7.0 / peak)
                part = (level - jnp.round(level)).astype(jnp.bfloat16)
                square = part * part
                series = (square + jnp.bfloat16(LINEAR)) * square + jnp.bfloat16(CONSTANT)
                wave = series * (jnp.bfloat16(0.25) - square) * part
                wave = wave * (peak * (GAIN / 7.0)).astype(jnp.bfloat16)
                waves[half, ratio, spot, group * GROUP : (group + 1) * GROUP, :] = wave

    def multiply(half, first):
        for ratio in range(RATIOS):
            left = []
            for group in range(groups):
                shrink = scales[first + group, RATIOS + ratio : RATIOS + ratio + 1, :]
                left.append(normed[first + group] * shrink.astype(jnp.bfloat16))
            right = jnp.concatenate([waves[half, ratio, spot] for spot in range(len(parts))], axis=1)
            delta[ratio] += jnp.dot(jnp.concatenate(left, axis=1), right, preferred_element_type=jnp.float32)

    def project_exact(half, first, slot):
        left = jnp.concatenate([normed[first + group] for group in range(groups)], axis=1)
        right = [held[slot, spot, half * HALF : (half + 1) * HALF, :] for spot in range(len(parts))]
        exact[...] += jnp.dot(left, jnp.concatenate(right, axis=1), preferred_element_type=jnp.float32)

    for fetch in fetches(0):
        fetch.start()
    for slot in range(count):
        owner = me[0] ^ slot
        for piece in range(per_slot):
            means[pl.ds(owner * per_slot + piece, 1), :] = totals[slot][piece : piece + 1, :]
    sums_all = means[...]
    logged = jnp.log(sums_all + 1e-06)
    centred = logged - 0.5 * (jnp.max(logged) + jnp.min(logged))
    means[...] = sums_all / tokens
    for ratio in range(RATIOS):
        alpha = ids[ratio].astype(jnp.float32) / GRID
        scale = jnp.exp(alpha * centred)
        scales[:, ratio, :] = scale
        scales[:, RATIOS + ratio, :] = 1.0 / scale
    exact[...] = jnp.zeros_like(exact)
    delta[...] = jnp.zeros_like(delta)
    waves[1] = jnp.zeros_like(waves[1])
    prepare(0, 0)

    @pl.loop(0, steps)
    def _(step):
        base = step * 2 * groups
        slot = lax.rem(step, 2)

        @pl.when(step + 1 < steps)
        def _():
            for fetch in fetches(step + 1):
                fetch.start()

        for fetch in fetches(step):
            fetch.wait()
        for half in range(2):
            first = base + half * groups
            for group in range(groups):
                index = half * groups + group
                prepare(jnp.minimum(base + index + 1, blocks - 1), (index + 1) % 2)
                quantize(half, group, index % 2, slot)
            multiply(1 - half, jnp.maximum(first - groups, 0))
            project_exact(half, first, slot)

    multiply(1, blocks - groups)
    masks = [column(live[:, top : top + LANES]) for top in range(0, rows, LANES)]
    for ratio in range(RATIOS + 1):
        gathered = jnp.zeros((1, LANES), jnp.float32)
        for index, top in enumerate(range(0, rows, LANES)):
            for at in range(0, exact.shape[1], LANES):
                if ratio < RATIOS:
                    value = delta[ratio, top : top + LANES, at : at + LANES]
                else:
                    value = exact[top : top + LANES, at : at + LANES]
                value = value * masks[index]
                gathered = gathered + jnp.sum(value * value, axis=0, keepdims=True)
        sums[ratio : ratio + 1, :] = gathered
    sums[RATIOS + 1 :, :] = jnp.zeros((8 - RATIOS - 1, LANES), jnp.float32)


def blend_kernel(first, second, exact, delta, losses, query, kv):
    sums = first[...] + second[...]
    folded = [jnp.sum(sums[ratio : ratio + 1, :], axis=1, keepdims=True) for ratio in range(RATIOS + 1)]
    loss = [folded[ratio] / folded[RATIOS] for ratio in range(RATIOS)]
    inverse = [1.0 / (value * value) for value in loss]
    whole = inverse[0]
    for ratio in range(1, RATIOS):
        whole = whole + inverse[ratio]
    blended = exact[...]
    for ratio in range(RATIOS):
        losses[ratio] = loss[ratio][0, 0]
        blended = blended - (inverse[ratio] / whole) * delta[ratio]
    blended = blended.astype(jnp.bfloat16)
    query[...] = blended[:, : query.shape[1]]
    kv[...] = blended[:, query.shape[1] :]


SCALAR = pl.BlockSpec(memory_space=pltpu.SMEM)
VECTOR = pl.BlockSpec(memory_space=pltpu.VMEM)


def room(mebibytes):
    return pltpu.CompilerParams(vmem_limit_bytes=mebibytes << 20)


def cost(flops, moved):
    return pl.CostEstimate(flops=flops, bytes_accessed=moved, transcendentals=0)


def project(me, ratio_ids, live, total_slots, normed, q_weight, kv_weight, tokens):
    blocks, rows, _ = normed.shape
    features = blocks * LANES
    columns = q_weight.shape[1] + kv_weight.shape[1]
    spots = columns // LANES
    count = len(total_slots)
    return pl.pallas_call(
        functools.partial(project_kernel, count, tokens),
        in_specs=[SCALAR, SCALAR] + [VECTOR] * (2 + count) + [pl.BlockSpec(memory_space=pl.ANY)] * 2,
        out_specs=[VECTOR] * 4,
        out_shape=[
            jax.ShapeDtypeStruct((rows, columns), jnp.float32),
            jax.ShapeDtypeStruct((RATIOS, rows, columns), jnp.float32),
            jax.ShapeDtypeStruct((8, LANES), jnp.float32),
            jax.ShapeDtypeStruct((blocks, LANES), jnp.float32),
        ],
        scratch_shapes=[
            pltpu.VMEM((blocks, 8, LANES), jnp.float32),
            pltpu.VMEM((2, LANES, 8), jnp.float32),
            pltpu.VMEM((2, RATIOS, LANES, LANES), jnp.float32),
            pltpu.VMEM((2, RATIOS, spots, HALF, LANES), jnp.bfloat16),
            pltpu.VMEM((2, spots, 2 * HALF, LANES), jnp.bfloat16),
            pltpu.SemaphoreType.DMA((2, spots)),
        ],
        compiler_params=room(50),
        cost_estimate=cost(10 * rows * features * columns, 8 * features * columns),
        name="project",
    )(me, ratio_ids, live, *total_slots, normed, q_weight, kv_weight)


def per_device(hidden, live, norm_gain, q_weight, kv_weight, ratio_ids):
    rows, width = hidden.shape
    shards = lax.axis_size("mp")
    features = width * shards
    tokens = rows * lax.axis_size("dp")
    query, kv = q_weight.shape[1], kv_weight.shape[1]
    me = lax.axis_index("mp").reshape(1).astype(jnp.int32)

    squares, hidden, live_row, gain = pl.pallas_call(
        squares_kernel,
        in_specs=[VECTOR] * 3,
        out_specs=[VECTOR] * 4,
        out_shape=[
            jax.ShapeDtypeStruct((1, rows), jnp.float32),
            jax.ShapeDtypeStruct(hidden.shape, hidden.dtype),
            jax.ShapeDtypeStruct((1, rows), jnp.float32),
            jax.ShapeDtypeStruct((features // LANES, LANES), jnp.float32),
        ],
        compiler_params=room(2),
        cost_estimate=cost(2 * rows * width, 4 * rows * width),
        name="squares",
    )(hidden, live.reshape(1, rows), norm_gain.reshape(features // LANES, LANES))
    squares = sum(peers(squares, "mp"))
    squares, late = lax.optimization_barrier((squares, hidden))
    *nearer, farthest = distances("mp")
    held = {0: late, farthest: swap(late, "mp", farthest)}
    for distance in nearer:
        held[distance] = swap(late, "mp", distance)
    sums = pl.pallas_call(
        functools.partial(stats_kernel, features),
        in_specs=[SCALAR] + [VECTOR] * 4,
        out_specs=VECTOR,
        out_shape=jax.ShapeDtypeStruct((width // LANES, LANES), jnp.float32),
        compiler_params=room(2),
        cost_estimate=cost(8 * rows * width, 2 * rows * width),
        name="stats",
    )(me, squares, live_row, gain, hidden)
    sums = total(sums, "dp")
    sums, held[farthest] = lax.optimization_barrier((sums, held[farthest]))
    total_slots = peers(sums, "mp")
    for distance in reversed(nearer):
        for place, block in list(held.items()):
            if place ^ distance not in held:
                held[place ^ distance] = swap(block, "mp", distance)
    hidden_slots = [held[place] for place in range(shards)]
    normed = pl.pallas_call(
        functools.partial(norm_kernel, features),
        in_specs=[SCALAR] + [VECTOR] * (2 + shards),
        out_specs=VECTOR,
        out_shape=jax.ShapeDtypeStruct((features // LANES, rows, LANES), jnp.bfloat16),
        compiler_params=room(2),
        cost_estimate=cost(4 * rows * features, 4 * rows * features),
        name="norm",
    )(me, squares, gain, *hidden_slots)
    exact, delta, sums, means = project(
        me, ratio_ids, live_row, total_slots, normed, q_weight, kv_weight, float(tokens)
    )
    sums = sum(peers(sums, "mp"))
    *steps, final = distances("dp")
    for distance in steps:
        sums = sums + swap(sums, "dp", distance)
    losses, q_latent, kv_latent = pl.pallas_call(
        blend_kernel,
        in_specs=[VECTOR] * 4,
        out_shape=[
            jax.ShapeDtypeStruct((RATIOS,), jnp.float32),
            jax.ShapeDtypeStruct((rows, query), jnp.bfloat16),
            jax.ShapeDtypeStruct((rows, kv), jnp.bfloat16),
        ],
        out_specs=[SCALAR, VECTOR, VECTOR],
        compiler_params=room(2),
        cost_estimate=cost(10 * rows * (query + kv), 24 * rows * (query + kv)),
        name="blend",
    )(sums, swap(sums, "dp", final), exact, delta)
    return losses, q_latent, kv_latent, means.reshape(features)


def solution(mesh):
    placed = (P("dp", "mp"), P("dp"), P(), P(None, "mp"), P(None, "mp"), P())
    return jax.shard_map(
        per_device,
        mesh=mesh,
        in_specs=placed,
        out_specs=(P(), P("dp", "mp"), P("dp", "mp"), P()),
        check_vma=False,
    )
```

time: 91.1 us -> 77.9 us (0.86)
  Pallas kernels: 41.5 us -> 35.7 us
  other arithmetic: 3.85 us -> 0.03 us
  waiting for transfers between devices: 22.6 us -> 19.7 us
    pallas_call x3 -> x5, Pallas kernels: 41.5 us -> 35.7 us  [the longest x1 33.5 us: project(): pl.pallas_call(functools.partial(project_kernel, count, tokens), in_specs...]
    ppermute x18, waiting for transfers between devices: 22.6 us -> 19.7 us  [swap(): return lax.ppermute(x, axis, [(i, i ^ distance) for i in range(size)])]
    reduce_sum x2 -> x0, other arithmetic: 2.47 us -> none  [the longest x1 1.28 us: per_device(): sums = jnp.sum(jnp.abs(own.astype(jnp.float32)) * live_rows, axis=0)]
    unnamed x20 -> x8, local copies, waits for them, and re-layouts: 2.11 us -> 2.42 us
  transfers between devices with their start and end apart: 18 -> 18, of which waited for: 10 -> 12; matrix products, arithmetic and copies ran while one was open for 3% -> 0% of each run, Pallas kernels for 4% -> 1%
where the time goes in v3:
time: 77.9 us; the launch traced here: 77.7 us
  Pallas kernels  35.7 us (46%)
  waiting for transfers between devices  19.7 us (25%)
  starting transfers between devices  19.2 us (25%)
  local copies, waits for them, and re-layouts  2.42 us (3%)
    pallas_call x1, Pallas kernels, project(): pl.pallas_call(functools.partial(project_kernel, count, tokens), in_specs...  33.5 us
    ppermute x18, waiting for transfers between devices, swap(): return lax.ppermute(x, axis, [(i, i ^ distance) for i in range(size)])  19.7 us
    ppermute x18, starting transfers between devices, swap(): return lax.ppermute(x, axis, [(i, i ^ distance) for i in range(size)])  19.2 us
    unnamed x8, local copies, waits for them, and re-layouts  2.42 us
  transfers between devices with their start and end apart: 18, of which 12 were waited for; matrix products, arithmetic and copies ran while one was open for 0% of the time, Pallas kernels for 1%

profile of v3, /device:TPU:0, one launch (start us, length us, event | category | flops | bytes accessed | tf_op | source)
XLA Modules:
  0.0 77.7 jit_solution(8018098701701605555)
XLA Ops:
  0.6 0.0 copy-start
  0.6 1.0 %copy-done = bf16[128,1792]{1,0:T(8,128)(2,1)S(1)} copy-done((bf16[128,1792]{1,0:T(8,128)(2,1)S(1)}, bf16[128,1792]{1,0:T(8,128)(2,1)}, u32[]{:S(2)}) %copy-start) | copy-done | bytes 458776
  1.7 0.0 copy-start.1
  1.7 0.7 copy-done.1
  2.4 0.0 copy-start.2
  2.4 0.7 copy-done.2
  3.1 0.2 squares.1
  3.3 0.6 collective-permute-start
  3.8 2.6 %collective-permute-start.1 = (f32[1,128]{1,0:T(1,128)S(1)}, f32[1,128]{1,0:T(1,128)S(1)}, u32[]{:S(2)}, u32[]{:S(2)}) collective-permute-start(f32[1,128]{1,0:T(1,128)S(1)} %get-tuple-element.20), channel_id=1, source_target_pairs={{0,2},{1,3},{2,0},{3,1},{4,6},{5,7},{6,4},{7,5},{8,10},{9,11},{10,... | collective-permute-start | bytes 1544 | tf_op jit(solution)/shard_map/ppermute | solution.py:20
  6.4 0.0 collective-permute-start.2
  6.4 0.0 collective-permute-done
  6.4 1.5 %collective-permute-done.1 = f32[1,128]{1,0:T(1,128)S(1)} collective-permute-done((f32[1,128]{1,0:T(1,128)S(1)}, f32[1,128]{1,0:T(1,128)S(1)}, u32[]{:S(2)}, u32[]{:S(2)}) %collective-permute-start.1) | collective-permute-done | bytes 544 | tf_op jit(solution)/shard_map/ppermute | solution.py:20
  7.9 1.4 %collective-permute-done.2 = f32[1,128]{1,0:T(1,128)S(1)} collective-permute-done((f32[1,128]{1,0:T(1,128)S(1)}, f32[1,128]{1,0:T(1,128)S(1)}, u32[]{:S(2)}, u32[]{:S(2)}) %collective-permute-start.2) | collective-permute-done | bytes 544 | tf_op jit(solution)/shard_map/ppermute | solution.py:20
  9.4 0.6 collective-permute-start.6
  10.0 0.6 stats.1
  10.6 1.6 %collective-permute-start.3 = (f32[14,128]{1,0:T(8,128)S(1)}, f32[14,128]{1,0:T(8,128)S(1)}, u32[]{:S(2)}, u32[]{:S(2)}) collective-permute-start(f32[14,128]{1,0:T(8,128)S(1)} %stats.1), channel_id=1, source_target_pairs={{0,4},{4,0},{8,12},{12,8},{16,20},{20,16},{24,28},{28,24},{1,5},{5... | collective-permute-start | bytes 21512 | tf_op jit(solution)/shard_map/ppermute | solution.py:20
  12.2 2.1 %collective-permute-done.3 = f32[14,128]{1,0:T(8,128)S(1)} collective-permute-done((f32[14,128]{1,0:T(8,128)S(1)}, f32[14,128]{1,0:T(8,128)S(1)}, u32[]{:S(2)}, u32[]{:S(2)}) %collective-permute-start.3) | collective-permute-done | bytes 7200 | tf_op jit(solution)/shard_map/ppermute | solution.py:20
  14.3 1.6 %collective-permute-start.4 = (f32[14,128]{1,0:T(8,128)S(1)}, f32[14,128]{1,0:T(8,128)S(1)}, u32[]{:S(2)}, u32[]{:S(2)}) collective-permute-start(f32[14,128]{1,0:T(8,128)S(1)} %add.36), channel_id=1, source_target_pairs={{0,8},{4,12},{8,0},{12,4},{16,24},{20,28},{24,16},{28,20},{1,9},{5... | collective-permute-start | bytes 21512 | tf_op jit(solution)/shard_map/ppermute | solution.py:20
  15.9 2.1 %collective-permute-done.4 = f32[14,128]{1,0:T(8,128)S(1)} collective-permute-done((f32[14,128]{1,0:T(8,128)S(1)}, f32[14,128]{1,0:T(8,128)S(1)}, u32[]{:S(2)}, u32[]{:S(2)}) %collective-permute-start.4) | collective-permute-done | bytes 7200 | tf_op jit(solution)/shard_map/ppermute | solution.py:20
  17.9 2.6 %collective-permute-start.5 = (f32[14,128]{1,0:T(8,128)S(1)}, f32[14,128]{1,0:T(8,128)S(1)}, u32[]{:S(2)}, u32[]{:S(2)}) collective-permute-start(f32[14,128]{1,0:T(8,128)S(1)} %add.37), channel_id=1, source_target_pairs={{0,16},{4,20},{8,24},{12,28},{16,0},{20,4},{24,8},{28,12},{1,17},{... | collective-permute-start | bytes 21512 | tf_op jit(solution)/shard_map/ppermute | solution.py:20
  20.5 0.0 collective-permute-start.10
  20.5 2.0 %collective-permute-done.5 = f32[14,128]{1,0:T(8,128)S(1)} collective-permute-done((f32[14,128]{1,0:T(8,128)S(1)}, f32[14,128]{1,0:T(8,128)S(1)}, u32[]{:S(2)}, u32[]{:S(2)}) %collective-permute-start.5) | collective-permute-done | bytes 7200 | tf_op jit(solution)/shard_map/ppermute | solution.py:20
  22.5 0.0 copy-start.3
  22.5 0.0 collective-permute-done.6.refs_5_
  22.5 0.1 collective-permute-start.11
  22.6 0.5 collective-permute-start.7
  23.1 1.4 %collective-permute-start.8 = (f32[14,128]{1,0:T(8,128)S(1)}, f32[14,128]{1,0:T(8,128)S(1)}, u32[]{:S(2)}, u32[]{:S(2)}) collective-permute-start(f32[14,128]{1,0:T(8,128)S(1)} %add.38.refs_3_), channel_id=1, source_target_pairs={{0,2},{1,3},{2,0},{3,1},{4,6},{5,7},{6,4},{7,5},{8,10},{9,11},{10,... | collective-permute-start | bytes 21512 | tf_op jit(solution)/shard_map/ppermute | solution.py:20
  24.5 0.0 collective-permute-start.9
  24.5 0.0 collective-permute-done.10.refs_4_
  24.5 0.0 collective-permute-done.11.refs_6_
  24.5 0.5 norm.1.refs_7_
  25.0 0.0 collective-permute-done.7.refs_4_
  25.0 1.7 %collective-permute-done.8.refs_5_ = f32[14,128]{1,0:T(8,128)S(1)} collective-permute-done((f32[14,128]{1,0:T(8,128)S(1)}, f32[14,128]{1,0:T(8,128)S(1)}, u32[]{:S(2)}, u32[]{:S(2)}) %collective-permute-start.8) | collective-permute-done | bytes 7200 | tf_op jit(solution)/shard_map/ppermute | solution.py:20
  26.7 0.9 %collective-permute-done.9.refs_6_ = f32[14,128]{1,0:T(8,128)S(1)} collective-permute-done((f32[14,128]{1,0:T(8,128)S(1)}, f32[14,128]{1,0:T(8,128)S(1)}, u32[]{:S(2)}, u32[]{:S(2)}) %collective-permute-start.9) | collective-permute-done | bytes 7200 | tf_op jit(solution)/shard_map/ppermute | solution.py:20
  27.6 0.0 copy-done.3
  27.6 33.5 %project.1 = (f32[128,512]{1,0:T(8,128)S(1)}, f32[4,128,512]{2,1,0:T(8,128)S(1)}, f32[8,128]{1,0:T(8,128)S(1)}, f32[56,128]{1,0:T(8,128)}) custom-call(s32[1]{0:T(128)} %bitcast.me.refs_0_, s32[4]{0:T(128)S(1)} %copy-done.3, f32[1,128]{1,0:T(1,128)S(1)} %get-tuple-element.19.live.refs_2_, f32[14,128]{1,0:T(8,128)S(1)} %add.38.refs_3_, ...), custom_call_target="tpu_custom_call" | custom-call | flops 4697620480 | bytes 29360128 | tf_op jit(solution)/shard_map/project/pallas_call | solution.py:233
  61.1 0.2 collective-permute-start.12
  61.3 0.7 collective-permute-start.13
  62.0 1.1 %collective-permute-start.14 = (f32[8,128]{1,0:T(8,128)S(1)}, f32[8,128]{1,0:T(8,128)S(1)}, u32[]{:S(2)}, u32[]{:S(2)}) collective-permute-start(f32[8,128]{1,0:T(8,128)S(1)} %get-tuple-element.27), channel_id=1, source_target_pairs={{0,3},{1,2},{2,1},{3,0},{4,7},{5,6},{6,5},{7,4},{8,11},{9,10},{10,... | collective-permute-start | bytes 12296 | tf_op jit(solution)/shard_map/ppermute | solution.py:20
  63.1 0.0 collective-permute-done.12
  63.1 1.8 %collective-permute-done.13 = f32[8,128]{1,0:T(8,128)S(1)} collective-permute-done((f32[8,128]{1,0:T(8,128)S(1)}, f32[8,128]{1,0:T(8,128)S(1)}, u32[]{:S(2)}, u32[]{:S(2)}) %collective-permute-start.13) | collective-permute-done | bytes 4128 | tf_op jit(solution)/shard_map/ppermute | solution.py:20
  64.9 0.1 collective-permute-done.14
  65.0 1.5 %collective-permute-start.15 = (f32[8,128]{1,0:T(8,128)S(1)}, f32[8,128]{1,0:T(8,128)S(1)}, u32[]{:S(2)}, u32[]{:S(2)}) collective-permute-start(f32[8,128]{1,0:T(8,128)S(1)} %add_add_fusion), channel_id=1, source_target_pairs={{0,4},{4,0},{8,12},{12,8},{16,20},{20,16},{24,28},{28,24},{1,5},{5... | collective-permute-start | bytes 12296 | tf_op jit(solution)/shard_map/ppermute | solution.py:20
  66.5 2.1 %collective-permute-done.15 = f32[8,128]{1,0:T(8,128)S(1)} collective-permute-done((f32[8,128]{1,0:T(8,128)S(1)}, f32[8,128]{1,0:T(8,128)S(1)}, u32[]{:S(2)}, u32[]{:S(2)}) %collective-permute-start.15) | collective-permute-done | bytes 4128 | tf_op jit(solution)/shard_map/ppermute | solution.py:20
  68.6 1.6 %collective-permute-start.16 = (f32[8,128]{1,0:T(8,128)S(1)}, f32[8,128]{1,0:T(8,128)S(1)}, u32[]{:S(2)}, u32[]{:S(2)}) collective-permute-start(f32[8,128]{1,0:T(8,128)S(1)} %add.42), channel_id=1, source_target_pairs={{0,8},{4,12},{8,0},{12,4},{16,24},{20,28},{24,16},{28,20},{1,9},{5... | collective-permute-start | bytes 12296 | tf_op jit(solution)/shard_map/ppermute | solution.py:20
  70.2 2.0 %collective-permute-done.16 = f32[8,128]{1,0:T(8,128)S(1)} collective-permute-done((f32[8,128]{1,0:T(8,128)S(1)}, f32[8,128]{1,0:T(8,128)S(1)}, u32[]{:S(2)}, u32[]{:S(2)}) %collective-permute-start.16) | collective-permute-done | bytes 4128 | tf_op jit(solution)/shard_map/ppermute | solution.py:20
  72.2 2.6 %collective-permute-start.17 = (f32[8,128]{1,0:T(8,128)S(1)}, f32[8,128]{1,0:T(8,128)S(1)}, u32[]{:S(2)}, u32[]{:S(2)}) collective-permute-start(f32[8,128]{1,0:T(8,128)S(1)} %add.43.first), channel_id=1, source_target_pairs={{0,16},{4,20},{8,24},{12,28},{16,0},{20,4},{24,8},{28,12},{1,17},{... | collective-permute-start | bytes 12296 | tf_op jit(solution)/shard_map/ppermute | solution.py:20
  74.8 1.9 %collective-permute-done.17.second = f32[8,128]{1,0:T(8,128)S(1)} collective-permute-done((f32[8,128]{1,0:T(8,128)S(1)}, f32[8,128]{1,0:T(8,128)S(1)}, u32[]{:S(2)}, u32[]{:S(2)}) %collective-permute-start.17) | collective-permute-done | bytes 4128 | tf_op jit(solution)/shard_map/ppermute | solution.py:20
  76.8 0.9 %blend.1 = (f32[4]{0:T(128)}, bf16[128,384]{1,0:T(8,128)(2,1)}, bf16[128,128]{1,0:T(8,128)(2,1)}) custom-call(f32[8,128]{1,0:T(8,128)S(1)} %add.43.first, f32[8,128]{1,0:T(8,128)S(1)} %collective-permute-done.17.second, f32[128,512]{1,0:T(8,128)S(1)} %get-tuple-element.28.exact, f32[4,128,512]{2,1,0:T(8,128)S(1)} %get-tuple-element.29.delta), custom_call_target="tpu_custom_call" | custom-call | flops 655360 | bytes 1572864 | tf_op jit(solution)/shard_map/blend/pallas_call | solution.py:318
  (7 shorter events, 0.0 us)
Async XLA Ops:
  0.6 1.0 %copy-start = (bf16[128,1792]{1,0:T(8,128)(2,1)S(1)}, bf16[128,1792]{1,0:T(8,128)(2,1)}, u32[]{:S(2)}) copy-start(bf16[128,1792]{1,0:T(8,128)(2,1)} %hidden.1) | copy-start | bytes 1376260
  1.7 0.7 copy-start.1
  2.4 0.7 copy-start.2
  3.3 3.1 %collective-permute-start = (f32[1,128]{1,0:T(1,128)S(1)}, f32[1,128]{1,0:T(1,128)S(1)}, u32[]{:S(2)}, u32[]{:S(2)}) collective-permute-start(f32[1,128]{1,0:T(1,128)S(1)} %get-tuple-element.20), channel_id=1, source_target_pairs={{0,1},{1,0},{2,3},{3,2},{4,5},{5,4},{6,7},{7,6},{8,9},{9,8},{10,11... | collective-permute-start | bytes 1544 | tf_op jit(solution)/shard_map/ppermute | solution.py:20
  3.8 4.1 %collective-permute-start.1 = (f32[1,128]{1,0:T(1,128)S(1)}, f32[1,128]{1,0:T(1,128)S(1)}, u32[]{:S(2)}, u32[]{:S(2)}) collective-permute-start(f32[1,128]{1,0:T(1,128)S(1)} %get-tuple-element.20), channel_id=1, source_target_pairs={{0,2},{1,3},{2,0},{3,1},{4,6},{5,7},{6,4},{7,5},{8,10},{9,11},{10,... | collective-permute-start | bytes 1544 | tf_op jit(solution)/shard_map/ppermute | solution.py:20
  6.4 3.0 %collective-permute-start.2 = (f32[1,128]{1,0:T(1,128)S(1)}, f32[1,128]{1,0:T(1,128)S(1)}, u32[]{:S(2)}, u32[]{:S(2)}) collective-permute-start(f32[1,128]{1,0:T(1,128)S(1)} %get-tuple-element.20), channel_id=1, source_target_pairs={{0,3},{1,2},{2,1},{3,0},{4,7},{5,6},{6,5},{7,4},{8,11},{9,10},{10,... | collective-permute-start | bytes 1544 | tf_op jit(solution)/shard_map/ppermute | solution.py:20
  9.4 13.1 %collective-permute-start.6 = (bf16[128,1792]{1,0:T(8,128)(2,1)S(1)}, bf16[128,1792]{1,0:T(8,128)(2,1)S(1)}, u32[]{:S(2)}, u32[]{:S(2)}) collective-permute-start(bf16[128,1792]{1,0:T(8,128)(2,1)S(1)} %get-tuple-element.24.hidden.refs_3_), channel_id=1, source_target_pairs={{0,2},{1,3},{2,0},{3,1},{4,6},{5,7},{6,4},{7,5},{8,10},{9,11},{10,... | collective-permute-start | bytes 1376264 | tf_op jit(solution)/shard_map/ppermute | solution.py:20
  10.6 3.7 %collective-permute-start.3 = (f32[14,128]{1,0:T(8,128)S(1)}, f32[14,128]{1,0:T(8,128)S(1)}, u32[]{:S(2)}, u32[]{:S(2)}) collective-permute-start(f32[14,128]{1,0:T(8,128)S(1)} %stats.1), channel_id=1, source_target_pairs={{0,4},{4,0},{8,12},{12,8},{16,20},{20,16},{24,28},{28,24},{1,5},{5... | collective-permute-start | bytes 21512 | tf_op jit(solution)/shard_map/ppermute | solution.py:20
  14.3 3.7 %collective-permute-start.4 = (f32[14,128]{1,0:T(8,128)S(1)}, f32[14,128]{1,0:T(8,128)S(1)}, u32[]{:S(2)}, u32[]{:S(2)}) collective-permute-start(f32[14,128]{1,0:T(8,128)S(1)} %add.36), channel_id=1, source_target_pairs={{0,8},{4,12},{8,0},{12,4},{16,24},{20,28},{24,16},{28,20},{1,9},{5... | collective-permute-start | bytes 21512 | tf_op jit(solution)/shard_map/ppermute | solution.py:20
  17.9 4.5 %collective-permute-start.5 = (f32[14,128]{1,0:T(8,128)S(1)}, f32[14,128]{1,0:T(8,128)S(1)}, u32[]{:S(2)}, u32[]{:S(2)}) collective-permute-start(f32[14,128]{1,0:T(8,128)S(1)} %add.37), channel_id=1, source_target_pairs={{0,16},{4,20},{8,24},{12,28},{16,0},{20,4},{24,8},{28,12},{1,17},{... | collective-permute-start | bytes 21512 | tf_op jit(solution)/shard_map/ppermute | solution.py:20
  20.5 4.0 %collective-permute-start.10 = (bf16[128,1792]{1,0:T(8,128)(2,1)S(1)}, bf16[128,1792]{1,0:T(8,128)(2,1)S(1)}, u32[]{:S(2)}, u32[]{:S(2)}) collective-permute-start(bf16[128,1792]{1,0:T(8,128)(2,1)S(1)} %get-tuple-element.24.hidden.refs_3_), channel_id=1, source_target_pairs={{0,1},{1,0},{2,3},{3,2},{4,5},{5,4},{6,7},{7,6},{8,9},{9,8},{10,11... | collective-permute-start | bytes 1376264 | tf_op jit(solution)/shard_map/ppermute | solution.py:20
  22.5 5.1 %copy-start.3 = (s32[4]{0:T(128)S(1)}, s32[4]{0:T(128)}, u32[]{:S(2)}) copy-start(s32[4]{0:T(128)} %refs_1_.1) | copy-start | bytes 52
  22.5 2.0 %collective-permute-start.11 = (bf16[128,1792]{1,0:T(8,128)(2,1)S(1)}, bf16[128,1792]{1,0:T(8,128)(2,1)S(1)}, u32[]{:S(2)}, u32[]{:S(2)}) collective-permute-start(bf16[128,1792]{1,0:T(8,128)(2,1)S(1)} %collective-permute-done.6.refs_5_), channel_id=1, source_target_pairs={{0,1},{1,0},{2,3},{3,2},{4,5},{5,4},{6,7},{7,6},{8,9},{9,8},{10,11... | collective-permute-start | bytes 1376264 | tf_op jit(solution)/shard_map/ppermute | solution.py:20
  22.6 2.4 %collective-permute-start.7 = (f32[14,128]{1,0:T(8,128)S(1)}, f32[14,128]{1,0:T(8,128)S(1)}, u32[]{:S(2)}, u32[]{:S(2)}) collective-permute-start(f32[14,128]{1,0:T(8,128)S(1)} %add.38.refs_3_), channel_id=1, source_target_pairs={{0,1},{1,0},{2,3},{3,2},{4,5},{5,4},{6,7},{7,6},{8,9},{9,8},{10,11... | collective-permute-start | bytes 21512 | tf_op jit(solution)/shard_map/ppermute | solution.py:20
  23.1 3.7 %collective-permute-start.8 = (f32[14,128]{1,0:T(8,128)S(1)}, f32[14,128]{1,0:T(8,128)S(1)}, u32[]{:S(2)}, u32[]{:S(2)}) collective-permute-start(f32[14,128]{1,0:T(8,128)S(1)} %add.38.refs_3_), channel_id=1, source_target_pairs={{0,2},{1,3},{2,0},{3,1},{4,6},{5,7},{6,4},{7,5},{8,10},{9,11},{10,... | collective-permute-start | bytes 21512 | tf_op jit(solution)/shard_map/ppermute | solution.py:20
  24.5 3.1 %collective-permute-start.9 = (f32[14,128]{1,0:T(8,128)S(1)}, f32[14,128]{1,0:T(8,128)S(1)}, u32[]{:S(2)}, u32[]{:S(2)}) collective-permute-start(f32[14,128]{1,0:T(8,128)S(1)} %add.38.refs_3_), channel_id=1, source_target_pairs={{0,3},{1,2},{2,1},{3,0},{4,7},{5,6},{6,5},{7,4},{8,11},{9,10},{10,... | collective-permute-start | bytes 21512 | tf_op jit(solution)/shard_map/ppermute | solution.py:20
  61.1 1.9 %collective-permute-start.12 = (f32[8,128]{1,0:T(8,128)S(1)}, f32[8,128]{1,0:T(8,128)S(1)}, u32[]{:S(2)}, u32[]{:S(2)}) collective-permute-start(f32[8,128]{1,0:T(8,128)S(1)} %get-tuple-element.27), channel_id=1, source_target_pairs={{0,1},{1,0},{2,3},{3,2},{4,5},{5,4},{6,7},{7,6},{8,9},{9,8},{10,11... | collective-permute-start | bytes 12296 | tf_op jit(solution)/shard_map/ppermute | solution.py:20
  61.3 3.6 %collective-permute-start.13 = (f32[8,128]{1,0:T(8,128)S(1)}, f32[8,128]{1,0:T(8,128)S(1)}, u32[]{:S(2)}, u32[]{:S(2)}) collective-permute-start(f32[8,128]{1,0:T(8,128)S(1)} %get-tuple-element.27), channel_id=1, source_target_pairs={{0,2},{1,3},{2,0},{3,1},{4,6},{5,7},{6,4},{7,5},{8,10},{9,11},{10,... | collective-permute-start | bytes 12296 | tf_op jit(solution)/shard_map/ppermute | solution.py:20
  62.0 3.0 %collective-permute-start.14 = (f32[8,128]{1,0:T(8,128)S(1)}, f32[8,128]{1,0:T(8,128)S(1)}, u32[]{:S(2)}, u32[]{:S(2)}) collective-permute-start(f32[8,128]{1,0:T(8,128)S(1)} %get-tuple-element.27), channel_id=1, source_target_pairs={{0,3},{1,2},{2,1},{3,0},{4,7},{5,6},{6,5},{7,4},{8,11},{9,10},{10,... | collective-permute-start | bytes 12296 | tf_op jit(solution)/shard_map/ppermute | solution.py:20
  65.0 3.6 %collective-permute-start.15 = (f32[8,128]{1,0:T(8,128)S(1)}, f32[8,128]{1,0:T(8,128)S(1)}, u32[]{:S(2)}, u32[]{:S(2)}) collective-permute-start(f32[8,128]{1,0:T(8,128)S(1)} %add_add_fusion), channel_id=1, source_target_pairs={{0,4},{4,0},{8,12},{12,8},{16,20},{20,16},{24,28},{28,24},{1,5},{5... | collective-permute-start | bytes 12296 | tf_op jit(solution)/shard_map/ppermute | solution.py:20
  68.6 3.6 %collective-permute-start.16 = (f32[8,128]{1,0:T(8,128)S(1)}, f32[8,128]{1,0:T(8,128)S(1)}, u32[]{:S(2)}, u32[]{:S(2)}) collective-permute-start(f32[8,128]{1,0:T(8,128)S(1)} %add.42), channel_id=1, source_target_pairs={{0,8},{4,12},{8,0},{12,4},{16,24},{20,28},{24,16},{28,20},{1,9},{5... | collective-permute-start | bytes 12296 | tf_op jit(solution)/shard_map/ppermute | solution.py:20
  72.2 4.5 %collective-permute-start.17 = (f32[8,128]{1,0:T(8,128)S(1)}, f32[8,128]{1,0:T(8,128)S(1)}, u32[]{:S(2)}, u32[]{:S(2)}) collective-permute-start(f32[8,128]{1,0:T(8,128)S(1)} %add.43.first), channel_id=1, source_target_pairs={{0,16},{4,20},{8,24},{12,28},{16,0},{20,4},{24,8},{28,12},{1,17},{... | collective-permute-start | bytes 12296 | tf_op jit(solution)/shard_map/ppermute | solution.py:20

commit v4 on v3

--- a/solution.py
+++ b/solution.py
@@ -11,7 +11,7 @@
 GRID = 20
 RATIOS = 4
 LANES = 128
-HALF = 256
+HALF = 512
 LINEAR, CONSTANT, GAIN = -1.1640625, 0.458984375, 8.705
 
 
@@ -26,9 +26,14 @@
     return [1 << bit for bit in range(size.bit_length() - 1)]
 
 
+def rounds(axis):
+    masks = [[distance] for distance in distances(axis)]
+    return [[1, 2, 3]] + masks[2:] if len(masks) > 1 else masks
+
+
 def total(x, axis):
-    for distance in distances(axis):
-        x = x + swap(x, axis, distance)
+    for masks in rounds(axis):
+        x = x + sum(swap(x, axis, mask) for mask in masks)
     return x
 
 
@@ -40,16 +45,19 @@
     return jnp.transpose(jnp.broadcast_to(row, (LANES, LANES)))
 
 
-def squares_kernel(hidden, live, gain, squares, kept, mask, kept_gain):
+def squares_kernel(hidden, squares, kept):
     kept[...] = hidden[...]
-    kept_gain[...] = gain[...]
-    mask[...] = live[...].astype(jnp.float32)
     for top in range(0, hidden.shape[0], LANES):
         gathered = jnp.zeros((LANES, LANES), jnp.float32)
         for at in range(0, hidden.shape[1], LANES):
             values = hidden[top : top + LANES, at : at + LANES].astype(jnp.float32)
             gathered = gathered + values * values
         squares[:, top : top + LANES] = jnp.sum(jnp.transpose(gathered), axis=0, keepdims=True)
+
+
+def keep_kernel(squares, live, gain, mask, kept_gain):
+    kept_gain[...] = gain[...]
+    mask[...] = live[...].astype(jnp.float32)
 
 
 def stats_kernel(features, me, squares, live, gain, hidden, sums):
@@ -86,9 +94,9 @@
 def project_kernel(count, tokens, *refs):
     me, ids, live = refs[:3]
     totals = refs[3 : 3 + count]
-    normed, query, kv = refs[3 + count : 6 + count]
-    exact, delta, sums, means = refs[6 + count : 10 + count]
-    scales, table, stretched, waves, held, arrivals = refs[10 + count :]
+    normed, start_query, start_kv, query, kv = refs[3 + count : 8 + count]
+    exact, delta, sums, means = refs[8 + count : 12 + count]
+    scales, table, stretched, held, arrivals, waves = refs[12 + count :]
     rows = normed.shape[1]
     blocks = normed.shape[0]
     per_slot = blocks // count
@@ -138,8 +146,9 @@
         right = [held[slot, spot, half * HALF : (half + 1) * HALF, :] for spot in range(len(parts))]
         exact[...] += jnp.dot(left, jnp.concatenate(right, axis=1), preferred_element_type=jnp.float32)
 
-    for fetch in fetches(0):
-        fetch.start()
+    starts = [(ref, at) for ref in (start_query, start_kv) for at in range(0, ref.shape[1], LANES)]
+    for spot, (ref, at) in enumerate(starts):
+        held[0, spot] = ref[:, at : at + LANES]
     for slot in range(count):
         owner = me[0] ^ slot
         for piece in range(per_slot):
@@ -168,8 +177,11 @@
             for fetch in fetches(step + 1):
                 fetch.start()
 
-        for fetch in fetches(step):
-            fetch.wait()
+        @pl.when(step > 0)
+        def _():
+            for fetch in fetches(step):
+                fetch.wait()
+
         for half in range(2):
             first = base + half * groups
             for group in range(groups):
@@ -193,6 +205,13 @@
                 gathered = gathered + jnp.sum(value * value, axis=0, keepdims=True)
         sums[ratio : ratio + 1, :] = gathered
     sums[RATIOS + 1 :, :] = jnp.zeros((8 - RATIOS - 1, LANES), jnp.float32)
+
+
+def project_scoped(count, tokens, spots, *refs):
+    def run(waves):
+        project_kernel(count, tokens, *refs, waves)
+
+    pl.run_scoped(run, pltpu.VMEM((2, RATIOS, spots, HALF, LANES), jnp.bfloat16))
 
 
 def blend_kernel(first, second, exact, delta, losses, query, kv):
@@ -224,15 +243,15 @@
     return pl.CostEstimate(flops=flops, bytes_accessed=moved, transcendentals=0)
 
 
-def project(me, ratio_ids, live, total_slots, normed, q_weight, kv_weight, tokens):
+def project(me, ratio_ids, live, total_slots, normed, start, q_weight, kv_weight, tokens):
     blocks, rows, _ = normed.shape
     features = blocks * LANES
     columns = q_weight.shape[1] + kv_weight.shape[1]
     spots = columns // LANES
     count = len(total_slots)
     return pl.pallas_call(
-        functools.partial(project_kernel, count, tokens),
-        in_specs=[SCALAR, SCALAR] + [VECTOR] * (2 + count) + [pl.BlockSpec(memory_space=pl.ANY)] * 2,
+        functools.partial(project_scoped, count, tokens, spots),
+        in_specs=[SCALAR, SCALAR] + [VECTOR] * (4 + count) + [pl.BlockSpec(memory_space=pl.ANY)] * 2,
         out_specs=[VECTOR] * 4,
         out_shape=[
             jax.ShapeDtypeStruct((rows, columns), jnp.float32),
@@ -244,14 +263,13 @@
             pltpu.VMEM((blocks, 8, LANES), jnp.float32),
             pltpu.VMEM((2, LANES, 8), jnp.float32),
             pltpu.VMEM((2, RATIOS, LANES, LANES), jnp.float32),
-            pltpu.VMEM((2, RATIOS, spots, HALF, LANES), jnp.bfloat16),
             pltpu.VMEM((2, spots, 2 * HALF, LANES), jnp.bfloat16),
             pltpu.SemaphoreType.DMA((2, spots)),
         ],
-        compiler_params=room(50),
+        compiler_params=room(49),
         cost_estimate=cost(10 * rows * features * columns, 8 * features * columns),
         name="project",
-    )(me, ratio_ids, live, *total_slots, normed, q_weight, kv_weight)
+    )(me, ratio_ids, live, *total_slots, normed, *start, q_weight, kv_weight)
 
 
 def per_device(hidden, live, norm_gain, q_weight, kv_weight, ratio_ids):
@@ -262,21 +280,32 @@
     query, kv = q_weight.shape[1], kv_weight.shape[1]
     me = lax.axis_index("mp").reshape(1).astype(jnp.int32)
 
-    squares, hidden, live_row, gain = pl.pallas_call(
+    squares, hidden = pl.pallas_call(
         squares_kernel,
-        in_specs=[VECTOR] * 3,
-        out_specs=[VECTOR] * 4,
+        in_specs=[VECTOR],
+        out_specs=[VECTOR] * 2,
         out_shape=[
             jax.ShapeDtypeStruct((1, rows), jnp.float32),
             jax.ShapeDtypeStruct(hidden.shape, hidden.dtype),
+        ],
+        compiler_params=room(2),
+        cost_estimate=cost(2 * rows * width, 4 * rows * width),
+        name="squares",
+    )(hidden)
+    live_row, gain = pl.pallas_call(
+        keep_kernel,
+        in_specs=[VECTOR] * 3,
+        out_specs=[VECTOR] * 2,
+        out_shape=[
             jax.ShapeDtypeStruct((1, rows), jnp.float32),
             jax.ShapeDtypeStruct((features // LANES, LANES), jnp.float32),
         ],
         compiler_params=room(2),
         cost_estimate=cost(2 * rows * width, 4 * rows * width),
-        name="squares",
-    )(hidden, live.reshape(1, rows), norm_gain.reshape(features // LANES, LANES))
-    squares = sum(peers(squares, "mp"))
+        name="keep",
+    )(squares, live.reshape(1, rows), norm_gain.reshape(features // LANES, LANES))
+    parts, live_row, gain = lax.optimization_barrier((peers(squares, "mp"), live_row, gain))
+    squares = sum(parts)
     squares, late = lax.optimization_barrier((squares, hidden))
     *nearer, farthest = distances("mp")
     held = {0: late, farthest: swap(late, "mp", farthest)}
@@ -291,8 +320,16 @@
         cost_estimate=cost(8 * rows * width, 2 * rows * width),
         name="stats",
     )(me, squares, live_row, gain, hidden)
-    sums = total(sums, "dp")
-    sums, held[farthest] = lax.optimization_barrier((sums, held[farthest]))
+    first, *others = rounds("dp")
+    sums = sums + sum(swap(sums, "dp", mask) for mask in first)
+    for distance in nearer:
+        sums, held[distance] = lax.optimization_barrier((sums, held[distance]))
+    for masks in others:
+        sums = sums + sum(swap(sums, "dp", mask) for mask in masks)
+    block = 2 * HALF
+    sums, held[farthest], *start = lax.optimization_barrier(
+        (sums, held[farthest], q_weight[:block], kv_weight[:block])
+    )
     total_slots = peers(sums, "mp")
     for distance in reversed(nearer):
         for place, block in list(held.items()):
@@ -309,12 +346,12 @@
         name="norm",
     )(me, squares, gain, *hidden_slots)
     exact, delta, sums, means = project(
-        me, ratio_ids, live_row, total_slots, normed, q_weight, kv_weight, float(tokens)
+        me, ratio_ids, live_row, total_slots, normed, start, q_weight, kv_weight, float(tokens)
     )
     sums = sum(peers(sums, "mp"))
-    *steps, final = distances("dp")
-    for distance in steps:
-        sums = sums + swap(sums, "dp", distance)
+    *steps, final = rounds("dp")
+    for masks in steps:
+        sums = sums + sum(swap(sums, "dp", mask) for mask in masks)
     losses, q_latent, kv_latent = pl.pallas_call(
         blend_kernel,
         in_specs=[VECTOR] * 4,
@@ -327,7 +364,7 @@
         compiler_params=room(2),
         cost_estimate=cost(10 * rows * (query + kv), 24 * rows * (query + kv)),
         name="blend",
-    )(sums, swap(sums, "dp", final), exact, delta)
+    )(sums, sum(swap(sums, "dp", mask) for mask in final), exact, delta)
     return losses, q_latent, kv_latent, means.reshape(features)
 
 

time: 77.9 us -> 70 us (0.90)
  Pallas kernels: 35.7 us -> 29.5 us
  waiting for transfers between devices: 19.7 us -> 14.5 us
  local copies, waits for them, and re-layouts: 2.42 us -> 4.6 us
  starting transfers between devices: 19.2 us -> 20.4 us
    pallas_call x2 -> x3, Pallas kernels: 33.7 us -> 27.6 us  [the longest x1 27.4 us: project(): pl.pallas_call(functools.partial(project_scoped, count, tokens, spots), i...]
    ppermute x18 -> x20, waiting for transfers between devices: 19.7 us -> 14.5 us  [swap(): return lax.ppermute(x, axis, [(i, i ^ distance) for i in range(size)])]
    slice x0 -> x2, local copies, waits for them, and re-layouts: none -> 2.18 us  [the longest x1 1.21 us: per_device(): q_weight[:block]]
    ppermute x18 -> x20, starting transfers between devices: 19.2 us -> 20.4 us  [swap(): return lax.ppermute(x, axis, [(i, i ^ distance) for i in range(size)])]
  transfers between devices with their start and end apart: 18 -> 20, of which waited for: 12 -> 12; matrix products, arithmetic and copies ran while one was open for 0% -> 3% of each run, Pallas kernels for 1% -> 2%
where the time goes in v4:
time: 70 us; the launch traced here: 69.7 us
  Pallas kernels  29.5 us (42%)
  starting transfers between devices  20.4 us (29%)
  waiting for transfers between devices  14.5 us (21%)
  local copies, waits for them, and re-layouts  4.6 us (7%)
  between operations  0.73 us (1%)
    pallas_call x1, Pallas kernels, project(): pl.pallas_call(functools.partial(project_scoped, count, tokens, spots), i...  27.4 us
    ppermute x20, starting transfers between devices, swap(): return lax.ppermute(x, axis, [(i, i ^ distance) for i in range(size)])  20.4 us
    ppermute x20, waiting for transfers between devices, swap(): return lax.ppermute(x, axis, [(i, i ^ distance) for i in range(size)])  14.5 us
    unnamed x8, local copies, waits for them, and re-layouts  2.42 us
  transfers between devices with their start and end apart: 20, of which 12 were waited for; matrix products, arithmetic and copies ran while one was open for 3% of the time, Pallas kernels for 2%

profile of v4, /device:TPU:0, one launch (start us, length us, event | category | flops | bytes accessed | tf_op | source)
XLA Modules:
  0.0 69.7 jit_solution(8794643011765047840)
XLA Ops:
  0.6 0.0 copy-start
  0.6 1.0 %copy-done = bf16[128,1792]{1,0:T(8,128)(2,1)S(1)} copy-done((bf16[128,1792]{1,0:T(8,128)(2,1)S(1)}, bf16[128,1792]{1,0:T(8,128)(2,1)}, u32[]{:S(2)}) %copy-start) | copy-done | bytes 458776
  1.6 0.2 squares.1
  1.8 0.6 collective-permute-start
  2.4 2.6 %collective-permute-start.1 = (f32[1,128]{1,0:T(1,128)S(1)}, f32[1,128]{1,0:T(1,128)S(1)}, u32[]{:S(2)}, u32[]{:S(2)}) collective-permute-start(f32[1,128]{1,0:T(1,128)S(1)} %get-tuple-element.33.squares), channel_id=1, source_target_pairs={{0,2},{1,3},{2,0},{3,1},{4,6},{5,7},{6,4},{7,5},{8,10},{9,11},{10,... | collective-permute-start | bytes 1544 | tf_op jit(solution)/shard_map/ppermute | solution.py:20
  5.0 0.0 collective-permute-start.2
  5.0 0.0 copy-start.1
  5.0 0.7 %copy-done.1 = f32[7168]{0:T(1024)S(1)} copy-done((f32[7168]{0:T(1024)S(1)}, f32[7168]{0:T(1024)}, u32[]{:S(2)}) %copy-start.1) | copy-done | bytes 28696
  5.7 0.0 copy-start.2
  5.7 0.7 copy-done.2
  6.4 0.0 collective-permute-done
  6.4 0.1 collective-permute-done.1
  6.5 1.4 %collective-permute-done.2 = f32[1,128]{1,0:T(1,128)S(1)} collective-permute-done((f32[1,128]{1,0:T(1,128)S(1)}, f32[1,128]{1,0:T(1,128)S(1)}, u32[]{:S(2)}, u32[]{:S(2)}) %collective-permute-start.2) | collective-permute-done | bytes 544 | tf_op jit(solution)/shard_map/ppermute | solution.py:20
  8.0 0.2 collective-permute-start.6
  8.1 0.6 collective-permute-start.8
  8.7 0.6 stats.1
  9.2 1.6 %collective-permute-start.3 = (f32[14,128]{1,0:T(8,128)S(1)}, f32[14,128]{1,0:T(8,128)S(1)}, u32[]{:S(2)}, u32[]{:S(2)}) collective-permute-start(f32[14,128]{1,0:T(8,128)S(1)} %stats.1), channel_id=1, source_target_pairs={{0,4},{4,0},{8,12},{12,8},{16,20},{20,16},{24,28},{28,24},{1,5},{5... | collective-permute-start | bytes 21512 | tf_op jit(solution)/shard_map/ppermute | solution.py:20
  10.8 1.6 %collective-permute-start.4 = (f32[14,128]{1,0:T(8,128)S(1)}, f32[14,128]{1,0:T(8,128)S(1)}, u32[]{:S(2)}, u32[]{:S(2)}) collective-permute-start(f32[14,128]{1,0:T(8,128)S(1)} %stats.1), channel_id=1, source_target_pairs={{0,8},{4,12},{8,0},{12,4},{16,24},{20,28},{24,16},{28,20},{1,9},{5... | collective-permute-start | bytes 21512 | tf_op jit(solution)/shard_map/ppermute | solution.py:20
  12.4 0.4 collective-permute-start.5
  12.8 0.2 collective-permute-done.3
  13.0 1.5 %collective-permute-done.4 = f32[14,128]{1,0:T(8,128)S(1)} collective-permute-done((f32[14,128]{1,0:T(8,128)S(1)}, f32[14,128]{1,0:T(8,128)S(1)}, u32[]{:S(2)}, u32[]{:S(2)}) %collective-permute-start.4) | collective-permute-done | bytes 7200 | tf_op jit(solution)/shard_map/ppermute | solution.py:20
  14.5 2.5 %collective-permute-done.5 = f32[14,128]{1,0:T(8,128)S(1)} collective-permute-done((f32[14,128]{1,0:T(8,128)S(1)}, f32[14,128]{1,0:T(8,128)S(1)}, u32[]{:S(2)}, u32[]{:S(2)}) %collective-permute-start.5) | collective-permute-done | bytes 7200 | tf_op jit(solution)/shard_map/ppermute | solution.py:20
  17.0 0.0 collective-permute-done.6.refs_4_
  17.0 2.7 %collective-permute-start.7 = (f32[14,128]{1,0:T(8,128)S(1)}, f32[14,128]{1,0:T(8,128)S(1)}, u32[]{:S(2)}, u32[]{:S(2)}) collective-permute-start(f32[14,128]{1,0:T(8,128)S(1)} %add_add_fusion), channel_id=1, source_target_pairs={{0,16},{4,20},{8,24},{12,28},{16,0},{20,4},{24,8},{28,12},{1,17},{... | collective-permute-start | bytes 21512 | tf_op jit(solution)/shard_map/ppermute | solution.py:20
  19.6 1.2 %slice.6.refs_8_ = bf16[1024,384]{1,0:T(8,128)(2,1)S(1)} slice(bf16[7168,384]{1,0:T(8,128)(2,1)} %refs_10_.1), slice={[0:1024], [0:384]} | slice | bytes 1572864 | tf_op jit(solution)/shard_map/slice | solution.py:331
  20.8 1.0 %slice.7.refs_9_ = bf16[1024,128]{1,0:T(8,128)(2,1)S(1)} slice(bf16[7168,128]{1,0:T(8,128)(2,1)} %refs_11_.1), slice={[0:1024], [0:128]} | slice | bytes 524288 | tf_op jit(solution)/shard_map/slice | solution.py:331
  21.8 0.0 collective-permute-done.7
  21.8 0.0 copy-start.3
  21.8 0.0 collective-permute-done.8.refs_5_
  21.8 0.1 collective-permute-start.12
  21.9 1.5 %collective-permute-start.10 = (f32[14,128]{1,0:T(8,128)S(1)}, f32[14,128]{1,0:T(8,128)S(1)}, u32[]{:S(2)}, u32[]{:S(2)}) collective-permute-start(f32[14,128]{1,0:T(8,128)S(1)} %add.45.refs_3_), channel_id=1, source_target_pairs={{0,2},{1,3},{2,0},{3,1},{4,6},{5,7},{6,4},{7,5},{8,10},{9,11},{10,... | collective-permute-start | bytes 21512 | tf_op jit(solution)/shard_map/ppermute | solution.py:20
  23.4 0.3 collective-permute-start.11
  23.8 0.4 collective-permute-start.9
  24.1 0.0 collective-permute-done.12.refs_6_
  24.1 0.5 norm.1.refs_7_
  24.6 1.0 %collective-permute-done.10.refs_5_ = f32[14,128]{1,0:T(8,128)S(1)} collective-permute-done((f32[14,128]{1,0:T(8,128)S(1)}, f32[14,128]{1,0:T(8,128)S(1)}, u32[]{:S(2)}, u32[]{:S(2)}) %collective-permute-start.10) | collective-permute-done | bytes 7200 | tf_op jit(solution)/shard_map/ppermute | solution.py:20
  25.6 0.9 %collective-permute-done.11.refs_6_ = f32[14,128]{1,0:T(8,128)S(1)} collective-permute-done((f32[14,128]{1,0:T(8,128)S(1)}, f32[14,128]{1,0:T(8,128)S(1)}, u32[]{:S(2)}, u32[]{:S(2)}) %collective-permute-start.11) | collective-permute-done | bytes 7200 | tf_op jit(solution)/shard_map/ppermute | solution.py:20
  26.5 0.0 collective-permute-done.9.refs_4_
  26.5 0.0 copy-done.3
  26.5 27.4 %project.1 = (f32[128,512]{1,0:T(8,128)S(1)}, f32[4,128,512]{2,1,0:T(8,128)S(1)}, f32[8,128]{1,0:T(8,128)S(1)}, f32[56,128]{1,0:T(8,128)}) custom-call(s32[1]{0:T(128)} %bitcast.me.refs_0_, s32[4]{0:T(128)S(1)} %copy-done.3, f32[1,128]{1,0:T(1,128)S(1)} %get-tuple-element.32.live.refs_2_, f32[14,128]{1,0:T(8,128)S(1)} %add.45.refs_3_, ...), custom_call_target="tpu_custom_call" | custom-call | flops 4697620480 | bytes 29360128 | tf_op jit(solution)/shard_map/project/pallas_call | solution.py:252
  53.9 0.2 collective-permute-start.13
  54.1 0.6 collective-permute-start.14
  54.8 1.1 %collective-permute-start.15 = (f32[8,128]{1,0:T(8,128)S(1)}, f32[8,128]{1,0:T(8,128)S(1)}, u32[]{:S(2)}, u32[]{:S(2)}) collective-permute-start(f32[8,128]{1,0:T(8,128)S(1)} %get-tuple-element.47), channel_id=1, source_target_pairs={{0,3},{1,2},{2,1},{3,0},{4,7},{5,6},{6,5},{7,4},{8,11},{9,10},{10,... | collective-permute-start | bytes 12296 | tf_op jit(solution)/shard_map/ppermute | solution.py:20
  55.8 0.0 collective-permute-done.13
  55.8 1.9 %collective-permute-done.14 = f32[8,128]{1,0:T(8,128)S(1)} collective-permute-done((f32[8,128]{1,0:T(8,128)S(1)}, f32[8,128]{1,0:T(8,128)S(1)}, u32[]{:S(2)}, u32[]{:S(2)}) %collective-permute-start.14) | collective-permute-done | bytes 4128 | tf_op jit(solution)/shard_map/ppermute | solution.py:20
  57.7 0.0 collective-permute-done.15
  57.8 0.5 collective-permute-start.16
  58.3 1.5 %collective-permute-start.17 = (f32[8,128]{1,0:T(8,128)S(1)}, f32[8,128]{1,0:T(8,128)S(1)}, u32[]{:S(2)}, u32[]{:S(2)}) collective-permute-start(f32[8,128]{1,0:T(8,128)S(1)} %add_add_fusion.2), channel_id=1, source_target_pairs={{0,8},{4,12},{8,0},{12,4},{16,24},{20,28},{24,16},{28,20},{1,9},{5... | collective-permute-start | bytes 12296 | tf_op jit(solution)/shard_map/ppermute | solution.py:20
  59.8 1.5 %collective-permute-start.18 = (f32[8,128]{1,0:T(8,128)S(1)}, f32[8,128]{1,0:T(8,128)S(1)}, u32[]{:S(2)}, u32[]{:S(2)}) collective-permute-start(f32[8,128]{1,0:T(8,128)S(1)} %add_add_fusion.2), channel_id=1, source_target_pairs={{0,12},{4,8},{8,4},{12,0},{16,28},{20,24},{24,20},{28,16},{1,13},{... | collective-permute-start | bytes 12296 | tf_op jit(solution)/shard_map/ppermute | solution.py:20
  61.3 0.1 collective-permute-done.16
  61.4 0.5 collective-permute-done.17
  61.9 2.4 %collective-permute-done.18 = f32[8,128]{1,0:T(8,128)S(1)} collective-permute-done((f32[8,128]{1,0:T(8,128)S(1)}, f32[8,128]{1,0:T(8,128)S(1)}, u32[]{:S(2)}, u32[]{:S(2)}) %collective-permute-start.18) | collective-permute-done | bytes 4128 | tf_op jit(solution)/shard_map/ppermute | solution.py:20
  64.3 2.6 %collective-permute-start.19 = (f32[8,128]{1,0:T(8,128)S(1)}, f32[8,128]{1,0:T(8,128)S(1)}, u32[]{:S(2)}, u32[]{:S(2)}) collective-permute-start(f32[8,128]{1,0:T(8,128)S(1)} %add_add_fusion.1.first), channel_id=1, source_target_pairs={{0,16},{4,20},{8,24},{12,28},{16,0},{20,4},{24,8},{28,12},{1,17},{... | collective-permute-start | bytes 12296 | tf_op jit(solution)/shard_map/ppermute | solution.py:20
  66.9 1.9 %collective-permute-done.19.second = f32[8,128]{1,0:T(8,128)S(1)} collective-permute-done((f32[8,128]{1,0:T(8,128)S(1)}, f32[8,128]{1,0:T(8,128)S(1)}, u32[]{:S(2)}, u32[]{:S(2)}) %collective-permute-start.19) | collective-permute-done | bytes 4128 | tf_op jit(solution)/shard_map/ppermute | solution.py:20
  68.8 0.9 %blend.1 = (f32[4]{0:T(128)}, bf16[128,384]{1,0:T(8,128)(2,1)}, bf16[128,128]{1,0:T(8,128)(2,1)}) custom-call(f32[8,128]{1,0:T(8,128)S(1)} %add_add_fusion.1.first, f32[8,128]{1,0:T(8,128)S(1)} %collective-permute-done.19.second, f32[128,512]{1,0:T(8,128)S(1)} %get-tuple-element.48.exact, f32[4,128,512]{2,1,0:T(8,128)S(1)} %get-tuple-element.49.delta), custom_call_target="tpu_custom_call" | custom-call | flops 655360 | bytes 1572864 | tf_op jit(solution)/shard_map/blend/pallas_call | solution.py:355
  (6 shorter events, 0.0 us)
Async XLA Ops:
  0.6 1.0 %copy-start = (bf16[128,1792]{1,0:T(8,128)(2,1)S(1)}, bf16[128,1792]{1,0:T(8,128)(2,1)}, u32[]{:S(2)}) copy-start(bf16[128,1792]{1,0:T(8,128)(2,1)} %hidden.1) | copy-start | bytes 1376260
  1.8 4.6 %collective-permute-start = (f32[1,128]{1,0:T(1,128)S(1)}, f32[1,128]{1,0:T(1,128)S(1)}, u32[]{:S(2)}, u32[]{:S(2)}) collective-permute-start(f32[1,128]{1,0:T(1,128)S(1)} %get-tuple-element.33.squares), channel_id=1, source_target_pairs={{0,1},{1,0},{2,3},{3,2},{4,5},{5,4},{6,7},{7,6},{8,9},{9,8},{10,11... | collective-permute-start | bytes 1544 | tf_op jit(solution)/shard_map/ppermute | solution.py:20
  2.4 4.1 %collective-permute-start.1 = (f32[1,128]{1,0:T(1,128)S(1)}, f32[1,128]{1,0:T(1,128)S(1)}, u32[]{:S(2)}, u32[]{:S(2)}) collective-permute-start(f32[1,128]{1,0:T(1,128)S(1)} %get-tuple-element.33.squares), channel_id=1, source_target_pairs={{0,2},{1,3},{2,0},{3,1},{4,6},{5,7},{6,4},{7,5},{8,10},{9,11},{10,... | collective-permute-start | bytes 1544 | tf_op jit(solution)/shard_map/ppermute | solution.py:20
  5.0 3.0 %collective-permute-start.2 = (f32[1,128]{1,0:T(1,128)S(1)}, f32[1,128]{1,0:T(1,128)S(1)}, u32[]{:S(2)}, u32[]{:S(2)}) collective-permute-start(f32[1,128]{1,0:T(1,128)S(1)} %get-tuple-element.33.squares), channel_id=1, source_target_pairs={{0,3},{1,2},{2,1},{3,0},{4,7},{5,6},{6,5},{7,4},{8,11},{9,10},{10,... | collective-permute-start | bytes 1544 | tf_op jit(solution)/shard_map/ppermute | solution.py:20
  5.0 0.7 %copy-start.1 = (f32[7168]{0:T(1024)S(1)}, f32[7168]{0:T(1024)}, u32[]{:S(2)}) copy-start(f32[7168]{0:T(1024)} %param.8) | copy-start | bytes 86020
  5.7 0.7 copy-start.2
  8.0 9.0 %collective-permute-start.6 = (bf16[128,1792]{1,0:T(8,128)(2,1)S(1)}, bf16[128,1792]{1,0:T(8,128)(2,1)S(1)}, u32[]{:S(2)}, u32[]{:S(2)}) collective-permute-start(bf16[128,1792]{1,0:T(8,128)(2,1)S(1)} %get-tuple-element.40.hidden.refs_3_), channel_id=1, source_target_pairs={{0,1},{1,0},{2,3},{3,2},{4,5},{5,4},{6,7},{7,6},{8,9},{9,8},{10,11... | collective-permute-start | bytes 1376264 | tf_op jit(solution)/shard_map/ppermute | solution.py:20
  8.1 13.7 %collective-permute-start.8 = (bf16[128,1792]{1,0:T(8,128)(2,1)S(1)}, bf16[128,1792]{1,0:T(8,128)(2,1)S(1)}, u32[]{:S(2)}, u32[]{:S(2)}) collective-permute-start(bf16[128,1792]{1,0:T(8,128)(2,1)S(1)} %get-tuple-element.40.hidden.refs_3_), channel_id=1, source_target_pairs={{0,2},{1,3},{2,0},{3,1},{4,6},{5,7},{6,4},{7,5},{8,10},{9,11},{10,... | collective-permute-start | bytes 1376264 | tf_op jit(solution)/shard_map/ppermute | solution.py:20
  9.2 3.7 %collective-permute-start.3 = (f32[14,128]{1,0:T(8,128)S(1)}, f32[14,128]{1,0:T(8,128)S(1)}, u32[]{:S(2)}, u32[]{:S(2)}) collective-permute-start(f32[14,128]{1,0:T(8,128)S(1)} %stats.1), channel_id=1, source_target_pairs={{0,4},{4,0},{8,12},{12,8},{16,20},{20,16},{24,28},{28,24},{1,5},{5... | collective-permute-start | bytes 21512 | tf_op jit(solution)/shard_map/ppermute | solution.py:20
  10.8 3.7 %collective-permute-start.4 = (f32[14,128]{1,0:T(8,128)S(1)}, f32[14,128]{1,0:T(8,128)S(1)}, u32[]{:S(2)}, u32[]{:S(2)}) collective-permute-start(f32[14,128]{1,0:T(8,128)S(1)} %stats.1), channel_id=1, source_target_pairs={{0,8},{4,12},{8,0},{12,4},{16,24},{20,28},{24,16},{28,20},{1,9},{5... | collective-permute-start | bytes 21512 | tf_op jit(solution)/shard_map/ppermute | solution.py:20
  12.4 4.5 %collective-permute-start.5 = (f32[14,128]{1,0:T(8,128)S(1)}, f32[14,128]{1,0:T(8,128)S(1)}, u32[]{:S(2)}, u32[]{:S(2)}) collective-permute-start(f32[14,128]{1,0:T(8,128)S(1)} %stats.1), channel_id=1, source_target_pairs={{0,12},{4,8},{8,4},{12,0},{16,28},{20,24},{24,20},{28,16},{1,13},{... | collective-permute-start | bytes 21512 | tf_op jit(solution)/shard_map/ppermute | solution.py:20
  17.0 4.8 %collective-permute-start.7 = (f32[14,128]{1,0:T(8,128)S(1)}, f32[14,128]{1,0:T(8,128)S(1)}, u32[]{:S(2)}, u32[]{:S(2)}) collective-permute-start(f32[14,128]{1,0:T(8,128)S(1)} %add_add_fusion), channel_id=1, source_target_pairs={{0,16},{4,20},{8,24},{12,28},{16,0},{20,4},{24,8},{28,12},{1,17},{... | collective-permute-start | bytes 21512 | tf_op jit(solution)/shard_map/ppermute | solution.py:20
  21.8 4.7 %copy-start.3 = (s32[4]{0:T(128)S(1)}, s32[4]{0:T(128)}, u32[]{:S(2)}) copy-start(s32[4]{0:T(128)} %refs_1_.1) | copy-start | bytes 52
  21.8 2.3 %collective-permute-start.12 = (bf16[128,1792]{1,0:T(8,128)(2,1)S(1)}, bf16[128,1792]{1,0:T(8,128)(2,1)S(1)}, u32[]{:S(2)}, u32[]{:S(2)}) collective-permute-start(bf16[128,1792]{1,0:T(8,128)(2,1)S(1)} %collective-permute-done.8.refs_5_), channel_id=1, source_target_pairs={{0,1},{1,0},{2,3},{3,2},{4,5},{5,4},{6,7},{7,6},{8,9},{9,8},{10,11... | collective-permute-start | bytes 1376264 | tf_op jit(solution)/shard_map/ppermute | solution.py:20
  21.9 3.7 %collective-permute-start.10 = (f32[14,128]{1,0:T(8,128)S(1)}, f32[14,128]{1,0:T(8,128)S(1)}, u32[]{:S(2)}, u32[]{:S(2)}) collective-permute-start(f32[14,128]{1,0:T(8,128)S(1)} %add.45.refs_3_), channel_id=1, source_target_pairs={{0,2},{1,3},{2,0},{3,1},{4,6},{5,7},{6,4},{7,5},{8,10},{9,11},{10,... | collective-permute-start | bytes 21512 | tf_op jit(solution)/shard_map/ppermute | solution.py:20
  23.4 3.1 %collective-permute-start.11 = (f32[14,128]{1,0:T(8,128)S(1)}, f32[14,128]{1,0:T(8,128)S(1)}, u32[]{:S(2)}, u32[]{:S(2)}) collective-permute-start(f32[14,128]{1,0:T(8,128)S(1)} %add.45.refs_3_), channel_id=1, source_target_pairs={{0,3},{1,2},{2,1},{3,0},{4,7},{5,6},{6,5},{7,4},{8,11},{9,10},{10,... | collective-permute-start | bytes 21512 | tf_op jit(solution)/shard_map/ppermute | solution.py:20
  23.8 2.8 %collective-permute-start.9 = (f32[14,128]{1,0:T(8,128)S(1)}, f32[14,128]{1,0:T(8,128)S(1)}, u32[]{:S(2)}, u32[]{:S(2)}) collective-permute-start(f32[14,128]{1,0:T(8,128)S(1)} %add.45.refs_3_), channel_id=1, source_target_pairs={{0,1},{1,0},{2,3},{3,2},{4,5},{5,4},{6,7},{7,6},{8,9},{9,8},{10,11... | collective-permute-start | bytes 21512 | tf_op jit(solution)/shard_map/ppermute | solution.py:20
  53.9 1.9 %collective-permute-start.13 = (f32[8,128]{1,0:T(8,128)S(1)}, f32[8,128]{1,0:T(8,128)S(1)}, u32[]{:S(2)}, u32[]{:S(2)}) collective-permute-start(f32[8,128]{1,0:T(8,128)S(1)} %get-tuple-element.47), channel_id=1, source_target_pairs={{0,1},{1,0},{2,3},{3,2},{4,5},{5,4},{6,7},{7,6},{8,9},{9,8},{10,11... | collective-permute-start | bytes 12296 | tf_op jit(solution)/shard_map/ppermute | solution.py:20
  54.1 3.6 %collective-permute-start.14 = (f32[8,128]{1,0:T(8,128)S(1)}, f32[8,128]{1,0:T(8,128)S(1)}, u32[]{:S(2)}, u32[]{:S(2)}) collective-permute-start(f32[8,128]{1,0:T(8,128)S(1)} %get-tuple-element.47), channel_id=1, source_target_pairs={{0,2},{1,3},{2,0},{3,1},{4,6},{5,7},{6,4},{7,5},{8,10},{9,11},{10,... | collective-permute-start | bytes 12296 | tf_op jit(solution)/shard_map/ppermute | solution.py:20
  54.8 3.0 %collective-permute-start.15 = (f32[8,128]{1,0:T(8,128)S(1)}, f32[8,128]{1,0:T(8,128)S(1)}, u32[]{:S(2)}, u32[]{:S(2)}) collective-permute-start(f32[8,128]{1,0:T(8,128)S(1)} %get-tuple-element.47), channel_id=1, source_target_pairs={{0,3},{1,2},{2,1},{3,0},{4,7},{5,6},{6,5},{7,4},{8,11},{9,10},{10,... | collective-permute-start | bytes 12296 | tf_op jit(solution)/shard_map/ppermute | solution.py:20
  57.8 3.6 %collective-permute-start.16 = (f32[8,128]{1,0:T(8,128)S(1)}, f32[8,128]{1,0:T(8,128)S(1)}, u32[]{:S(2)}, u32[]{:S(2)}) collective-permute-start(f32[8,128]{1,0:T(8,128)S(1)} %add_add_fusion.2), channel_id=1, source_target_pairs={{0,4},{4,0},{8,12},{12,8},{16,20},{20,16},{24,28},{28,24},{1,5},{5... | collective-permute-start | bytes 12296 | tf_op jit(solution)/shard_map/ppermute | solution.py:20
  58.3 3.6 %collective-permute-start.17 = (f32[8,128]{1,0:T(8,128)S(1)}, f32[8,128]{1,0:T(8,128)S(1)}, u32[]{:S(2)}, u32[]{:S(2)}) collective-permute-start(f32[8,128]{1,0:T(8,128)S(1)} %add_add_fusion.2), channel_id=1, source_target_pairs={{0,8},{4,12},{8,0},{12,4},{16,24},{20,28},{24,16},{28,20},{1,9},{5... | collective-permute-start | bytes 12296 | tf_op jit(solution)/shard_map/ppermute | solution.py:20
  59.8 4.5 %collective-permute-start.18 = (f32[8,128]{1,0:T(8,128)S(1)}, f32[8,128]{1,0:T(8,128)S(1)}, u32[]{:S(2)}, u32[]{:S(2)}) collective-permute-start(f32[8,128]{1,0:T(8,128)S(1)} %add_add_fusion.2), channel_id=1, source_target_pairs={{0,12},{4,8},{8,4},{12,0},{16,28},{20,24},{24,20},{28,16},{1,13},{... | collective-permute-start | bytes 12296 | tf_op jit(solution)/shard_map/ppermute | solution.py:20
  64.3 4.5 %collective-permute-start.19 = (f32[8,128]{1,0:T(8,128)S(1)}, f32[8,128]{1,0:T(8,128)S(1)}, u32[]{:S(2)}, u32[]{:S(2)}) collective-permute-start(f32[8,128]{1,0:T(8,128)S(1)} %add_add_fusion.1.first), channel_id=1, source_target_pairs={{0,16},{4,20},{8,24},{12,28},{16,0},{20,4},{24,8},{28,12},{1,17},{... | collective-permute-start | bytes 12296 | tf_op jit(solution)/shard_map/ppermute | solution.py:20
